TPU v7x, 32 devices: a whole 2x2x4 slice. The times are simulated.
32 devices in a mesh: band: 4 (over y, x), ga: 8 (over z, core).
Axes of the slice: x: 2, y: 2, z: 4, core: 2. Of those that a mesh axis runs over, the one named last changes fastest.
Arguments:
- psi: float32 [4096, 4096], P('band', 'ga'), may hold values from -6 to 6
- lower: float32 [4096, 4096], P('band', 'ga'), as said below
Outputs:
- orthonormal: float32 [4096, 4096], P('band', 'ga')
- block_intersection: float32 [4096, 1024], P('band')
Inputs may be any that keep to these rules, and one draw needn't show every extreme that they name: lower is lower triangular with its diagonal between 1 and 2.
All inputs are finite; a program needn't handle non-finite values.
Results may differ from a plain program's by a relative error of at most 0.00022.
Values sent between devices are 32-bit elements; how exact they have to be, the bound alone decides.
No kernel may reach another device: no remote copies, remote signals or barrier semaphores. Data moves between devices by JAX's collectives and lax.ppermute only.
A program may use at most 64 MiB of HBM per device.

v0:
```python
import functools
import jax
import jax.numpy as jnp
from jax import lax
from jax.experimental import pallas as pl
from jax.experimental.pallas import tpu as pltpu
from jax.sharding import PartitionSpec as P


AXES = ("band", "ga")
F32, BF16 = jnp.float32, jnp.bfloat16
PIECES = 2
CHUNKS = 2
SUB = 256


def split(x):
    hi = x.astype(BF16)
    return hi, (x - hi.astype(F32)).astype(BF16)


def mm(a, b, dims=(((1,), (0,)), ((), ()))):
    dot = functools.partial(lax.dot_general, dimension_numbers=dims, preferred_element_type=F32)
    return dot(a[0], b[0]) + (dot(a[0], b[1]) + dot(a[1], b[0]))


def tile(i):
    return pl.ds(pl.multiple_of(i * SUB, SUB), SUB)


def loop(count, body):
    lax.fori_loop(0, count, lambda i, _: (body(i), 0)[1], 0)


def invert_kernel(l_ref, *refs):
    outs, o_ref = refs[:-1], refs[-1]
    band, ga = lax.axis_index("band"), lax.axis_index("ga")
    n, wide = l_ref.shape
    o_ref[...] = l_ref[...]

    @pl.when(ga // 2 == band)
    def _():
        first = (ga % 2) * wide
        row = lax.broadcasted_iota(jnp.int32, (SUB, SUB), 0)
        col = lax.broadcasted_iota(jnp.int32, (SUB, SUB), 1)
        spots = [
            (pl.ds(pl.multiple_of(first + i * SUB, SUB), SUB), pl.ds(i * SUB, SUB))
            for i in range(wide // SUB)
        ]
        for at in spots:
            t = l_ref[at]
            d = jnp.where(row == col, t, 0.0)
            rd = 1.0 / jnp.sum(d, axis=1, keepdims=True)
            cd = 1.0 / jnp.sum(d, axis=0, keepdims=True)
            pair = (row == col + 1) & (row % 2 == 1)
            o_ref[at] = jnp.where(row == col, rd, jnp.where(pair, -t * rd * cd, 0.0))

        def level(k):
            r, c = lax.shift_right_logical(row, k), lax.shift_right_logical(col, k)
            mask = (r == c + 1) & (r % 2 == 1)
            xs = [o_ref[at] for at in spots]
            ys = [split(x) for x in xs]
            mid = [mm(split(jnp.where(mask, l_ref[at], 0.0)), y) for at, y in zip(spots, ys)]
            for at, x, y, v in zip(spots, xs, ys, mid):
                o_ref[at] = x - mm(y, split(v))

        loop(SUB.bit_length() - 2, lambda k: level(k + 1))

    rows = n // len(outs)
    for i, out in enumerate(outs):
        out[...] = o_ref[pl.ds(i * rows, rows), :]


def pick_kernel(take_own, own_ref, *refs):
    got, o_ref = refs[:-1], refs[-1]
    mine = take_own(lax.axis_index("band"), lax.axis_index("ga"))

    @pl.when(mine)
    def _():
        o_ref[...] = own_ref[...]

    @pl.when(jnp.logical_not(mine))
    def _():
        value = got[0][...]
        for ref in got[1:]:
            value = value + ref[...]
        o_ref[...] = value


def pick(take_own, own, *got):
    return call(functools.partial(pick_kernel, take_own), own.shape, [own, *got], flops=own.size)


def fetch(blocks, lbuf, sem, core):
    wide = lbuf.shape[2] // 2
    copies = []
    for d, (mine, other) in enumerate(blocks):
        for pieces, side in ((mine, core), (other, 1 - core)):
            row = 0
            for piece in pieces:
                to = lbuf.at[d, pl.ds(row, piece.shape[0]), pl.ds(pl.multiple_of(side * wide, wide), wide)]
                copies.append(pltpu.make_async_copy(piece, to, sem.at[d]))
                row += piece.shape[0]
    return copies


def unflatten(refs, pieces):
    it = iter(refs)
    blocks = []
    while len(blocks) * 2 * pieces < len(refs):
        blocks.append(([next(it) for _ in range(pieces)], [next(it) for _ in range(pieces)]))
    return blocks


def product_update(o_ref, lbuf, d, yh, yl, k):
    n = lbuf.shape[1]
    depth = min(2 * SUB, n)

    def body(t):
        i, j = t // (n // depth), t % (n // depth)
        cols = pl.ds(pl.multiple_of(j * depth, depth), depth)
        part = mm(split(lbuf[d, tile(i), cols]), (yh[k, cols, :], yl[k, cols, :]))
        o_ref[tile(i), :] = o_ref[tile(i), :] - part

    loop(n // SUB * (n // depth), body)


def band_kernel(s, final, pieces, given, *refs):
    r_ref, y_refs, refs = refs[0], refs[1 : 1 + given], refs[1 + given :]
    nblocks = given + (1 if final else 0)
    blocks = unflatten(refs[: nblocks * 2 * pieces], pieces)
    o_ref, lbuf, yh, yl, sem = refs[nblocks * 2 * pieces :]
    band, core = lax.axis_index("band"), lax.axis_index("ga") % 2
    n = lbuf.shape[1]

    @pl.when(band == s)
    def _():
        copies = fetch(blocks, lbuf, sem, core)
        for copy in copies:
            copy.start()
        o_ref[...] = r_ref[...]
        for k in range(given):

            def spread(i):
                yh[k, tile(i), :], yl[k, tile(i), :] = split(y_refs[k][tile(i), :])

            loop(n // SUB, spread)
        for copy in copies:
            copy.wait()
        if given:
            loop(given, lambda k: product_update(o_ref, lbuf, k, yh, yl, k))
        if not final:
            return

        def step(i):
            y = mm(split(lbuf[given, tile(i), tile(i)]), split(o_ref[tile(i), :]))
            o_ref[tile(i), :] = y
            y = split(y)

            def below(j, _):
                o_ref[tile(j), :] = o_ref[tile(j), :] - mm(split(lbuf[given, tile(j), tile(i)]), y)
                return 0

            lax.fori_loop(i + 1, n // SUB, below, 0)

        loop(n // SUB, step)


def corner(t, count):
    i = sum((t >= k * (k + 1) // 2).astype(jnp.int32) for k in range(1, count))
    return i, t - i * (i + 1) // 2


def gram_kernel(y_ref, o_ref, yh, yl):
    n = y_ref.shape[0]

    def spread(i):
        yh[tile(i), :], yl[tile(i), :] = split(y_ref[tile(i), :])

    loop(n // SUB, spread)
    count = n // SUB

    def body(t):
        i, j = corner(t, count)
        a, b = (yh[tile(i), :], yl[tile(i), :]), (yh[tile(j), :], yl[tile(j), :])
        o_ref[tile(t), :] = mm(a, b, (((1,), (1,)), ((), ())))

    loop(count * (count + 1) // 2, body)


def unpack_kernel(scale, p_ref, o_ref):
    count = o_ref.shape[0] // SUB

    def body(t):
        i, j = corner(t, count)
        block = p_ref[tile(t), :] * scale
        o_ref[tile(j), tile(i)] = block.T
        o_ref[tile(i), tile(j)] = block

    loop(count * (count + 1) // 2, body)


VM = pl.BlockSpec(memory_space=pltpu.VMEM)
ANY = pl.BlockSpec(memory_space=pl.ANY)


def call(kernel, out_shape, vmem_args, any_args=(), scratch=(), flops=0):
    return pl.pallas_call(
        kernel,
        out_shape=jax.ShapeDtypeStruct(out_shape, F32),
        in_specs=[VM] * len(vmem_args) + [ANY] * len(any_args),
        out_specs=VM,
        scratch_shapes=list(scratch),
        compiler_params=pltpu.CompilerParams(vmem_limit_bytes=40 * 2**20),
        cost_estimate=pl.CostEstimate(
            flops=flops, bytes_accessed=4 * out_shape[0] * out_shape[1], transcendentals=0
        ),
    )(*vmem_args, *any_args)


def block_scratch(blocks, terms, n, wc):
    return [
        pltpu.VMEM((blocks, n, n), F32),
        pltpu.VMEM((max(terms, 1), n, wc), BF16),
        pltpu.VMEM((max(terms, 1), n, wc), BF16),
        pltpu.SemaphoreType.DMA((blocks,)),
    ]


def flat(blocks):
    return [piece for mine, other in blocks for piece in mine + other]


def pick_band(a, own, other):
    return pick(lambda band, ga: band == a, own, other)


def routes(s, nb):
    if nb == 4:
        return {0: [[(0, 1)], [(0, 2), (1, 3)]], 1: [[(1, 2)], [(1, 3)]], 2: [[(2, 3)]]}[s]
    return [[(s, b)] for b in range(s + 1, nb)]


def stages(nq):
    return nq.bit_length() - 1


def local(psi, lower):
    nb, ng = lax.axis_size("band"), lax.axis_size("ga")
    nq = ng // 2
    n, w = psi.shape
    band, ga = lax.axis_index("band"), lax.axis_index("ga")
    chip, core = ga // 2, ga % 2

    def shift(x, hops):
        pairs = [
            (b * ng + q * 2 + c, bb * ng + qq * 2 + cc)
            for (b, q, c), (bb, qq, cc) in hops
        ]
        return lax.ppermute(x, AXES, pairs)

    def swap(x, bands):
        return shift(
            x, [((b, q, c), (b, q, 1 - c)) for b in bands for q in range(nq) for c in range(2)]
        )

    rows = n // PIECES
    cut = lambda x: [x[i * rows : (i + 1) * rows] for i in range(PIECES)]
    ready = pl.pallas_call(
        invert_kernel,
        out_shape=[jax.ShapeDtypeStruct((rows, lower.shape[1]), F32)] * PIECES,
        in_specs=[VM],
        out_specs=[VM] * PIECES,
        scratch_shapes=[pltpu.VMEM(lower.shape, F32)],
        cost_estimate=pl.CostEstimate(flops=2**28, bytes_accessed=2**22, transcendentals=0),
    )(lower)
    plain = lax.optimization_barrier(cut(lower))

    source = [ready] + [plain] * (nb - 1)
    got = [[[] for _ in range(PIECES)] for _ in range(nb)]

    def merged(d, i):
        if not got[d][i]:
            return source[d][i]
        return pick(lambda band, ga: ga // 2 == band - d, source[d][i], *got[d][i])

    for t in range(stages(nq)):
        bit = nq >> (t + 1)
        for d in range(nb):
            for i in range(PIECES):
                hops = []
                for b in range(d, nb):
                    for q in range(nq):
                        if (q ^ (b - d)) & (2 * bit - 1) == 0:
                            for c in range(2):
                                if d or c * (n // 2) < (i + 1) * rows:
                                    hops.append(((b, q, c), (b, q ^ bit, c)))
                got[d][i].append(shift(merged(d, i), hops))
    blocks = []
    for d in range(nb):
        mine = [merged(d, i) for i in range(PIECES)]
        other = [swap(x, range(d, nb)) for x in mine]
        blocks.append((mine, other))

    wc = w // CHUNKS
    seen = [{} for _ in range(CHUNKS)]
    done = [[] for _ in range(CHUNKS)]

    def apply(s, final, rhs, x, ks):
        need = [blocks[s - k] for k in ks] + ([blocks[0]] if final else [])
        return call(
            lambda *refs: band_kernel(s, final, PIECES, len(ks), *refs),
            (n, wc),
            [rhs] + [seen[x][k, s] for k in ks],
            flat(need),
            block_scratch(len(need), len(ks), n, wc),
            6 * n * n * wc * (len(ks) + 1),
        )

    for s in range(nb):
        for x in range(CHUNKS):
            rhs = psi[:, x * wc : (x + 1) * wc]
            if s > 1:
                rhs = apply(s, False, rhs, x, list(range(s - 1)))
            solved = apply(s, True, rhs, x, [s - 1] if s else [])
            done[x].append(solved)
            have = {s: solved}
            for hops in routes(s, nb) if s + 1 < nb else []:
                give = None
                for a, _ in hops:
                    give = have[a] if give is None else pick_band(a, have[a], give)
                took = shift(
                    give,
                    [((a, q, c), (b, q, c)) for a, b in hops for q in range(nq) for c in range(2)],
                )
                for _, b in hops:
                    have[b] = seen[x][s, b] = took
    parts = []
    for x in range(CHUNKS):
        value = done[x][0]
        for s in range(1, nb):
            value = jnp.where(band == s, done[x][s], value)
        parts.append(value)
    full = jnp.concatenate(parts, axis=1)

    count = n // SUB
    tri = count * (count + 1) // 2 * SUB
    packed = call(
        gram_kernel,
        (tri, SUB),
        [full],
        scratch=[pltpu.VMEM((n, w), BF16), pltpu.VMEM((n, w), BF16)],
        flops=3 * n * n * w,
    )
    half = tri // 2
    mine = lax.dynamic_slice_in_dim(packed, core * half, half, 0)
    give = lax.dynamic_slice_in_dim(packed, (1 - core) * half, half, 0)
    mine = mine + swap(give, range(nb))
    part = half // nq
    away = lambda x, d: shift(
        x, [((b, q, c), (b, q ^ d, c)) for b in range(nb) for q in range(nq) for c in range(2)]
    )
    piece = lambda q: lax.dynamic_slice_in_dim(mine, q * part, part, 0)
    total = piece(chip)
    for d in range(1, nq):
        total = total + away(piece(chip ^ d), d)
    result = jnp.zeros((half, SUB), F32)
    result = lax.dynamic_update_slice_in_dim(result, total, chip * part, 0)
    for d in range(1, nq):
        result = lax.dynamic_update_slice_in_dim(result, away(total, d), (chip ^ d) * part, 0)
    theirs = swap(result, range(nb))
    whole = jnp.zeros((tri, SUB), F32)
    whole = lax.dynamic_update_slice_in_dim(whole, result, core * half, 0)
    whole = lax.dynamic_update_slice_in_dim(whole, theirs, (1 - core) * half, 0)
    inter = call(
        functools.partial(unpack_kernel, 1.0 / (w * ng)), (n, n), [whole], flops=4 * n * n
    )
    return (full, inter)


def solution(mesh):
    return jax.shard_map(
        local,
        mesh=mesh,
        in_specs=(P("band", "ga"), P("band", "ga")),
        out_specs=(P("band", "ga"), P("band", None)),
        check_vma=False,
    )
```

profile of v0, /device:TPU:15, one launch (start us, length us, event | category | flops | bytes accessed | tf_op | source)
XLA Modules:
  0.0 445.3 jit_solution(2223440648520579646)
XLA Ops:
  0.6 3.1 shard_map.41
  8.8 29.8 %collective-permute-done.2.refs_0_ = f32[512,512]{1,0:T(8,128)S(1)} collective-permute-done((f32[512,512]{1,0:T(8,128)}, f32[512,512]{1,0:T(8,128)S(1)}, u32[]{:S(2)}, u32[]{:S(2)}) %collective-permute-start.2) | collective-permute-done | bytes 1048608 | tf_op jit(solution)/shard_map/ppermute | solution.py:260
  38.6 1.4 collective-permute-start.3
  41.5 1.4 collective-permute-start.21
  42.8 1.4 collective-permute-start.23
  44.4 59.8 %collective-permute-done.3.refs_1_ = f32[512,512]{1,0:T(8,128)S(1)} collective-permute-done((f32[512,512]{1,0:T(8,128)S(1)}, f32[512,512]{1,0:T(8,128)S(1)}, u32[]{:S(2)}, u32[]{:S(2)}) %collective-permute-start.3) | collective-permute-done | bytes 1048608 | tf_op jit(solution)/shard_map/ppermute | solution.py:260
  105.1 12.8 %collective-permute-start.4 = (f32[512,512]{1,0:T(8,128)S(1)}, f32[512,512]{1,0:T(8,128)S(1)}, u32[]{:S(2)}, u32[]{:S(2)}) collective-permute-start(f32[512,512]{1,0:T(8,128)S(1)} %shard_map.43.refs_1_.refs_6_), channel_id=1, source_target_pairs={{0,1},{1,0},{2,3},{3,2},{4,5},{5,4},{6,7},{7,6},{8,9},{9,8},{10,11... | collective-permute-start | bytes 3145736 | tf_op jit(solution)/shard_map/ppermute | solution.py:260
  121.8 6.5 %collective-permute-start.22 = (f32[512,512]{1,0:T(8,128)S(1)}, f32[512,512]{1,0:T(8,128)}, u32[]{:S(2)}, u32[]{:S(2)}) collective-permute-start(f32[512,512]{1,0:T(8,128)S(1)} %shard_map.57), channel_id=1, source_target_pairs={{16,18},{17,19},{20,22},{21,23},{26,24},{27,25},{30,28},{31,29}} | collective-permute-start | bytes 3145736 | tf_op jit(solution)/shard_map/ppermute | solution.py:260
  128.2 1.3 collective-permute-start.24
  129.6 1.7 fusion
  131.3 14.6 %collective-permute-done.9.refs_1_ = f32[512,512]{1,0:T(8,128)S(1)} collective-permute-done((f32[512,512]{1,0:T(8,128)S(1)}, f32[512,512]{1,0:T(8,128)S(1)}, u32[]{:S(2)}, u32[]{:S(2)}) %collective-permute-start.9) | collective-permute-done | bytes 1048608 | tf_op jit(solution)/shard_map/ppermute | solution.py:260
  146.7 21.7 %collective-permute-done.11.refs_1_ = f32[512,512]{1,0:T(8,128)S(1)} collective-permute-done((f32[512,512]{1,0:T(8,128)S(1)}, f32[512,512]{1,0:T(8,128)S(1)}, u32[]{:S(2)}, u32[]{:S(2)}) %collective-permute-start.11) | collective-permute-done | bytes 1048608 | tf_op jit(solution)/shard_map/ppermute | solution.py:260
  173.0 21.7 %collective-permute-start.12 = (f32[512,512]{1,0:T(8,128)S(1)}, f32[512,512]{1,0:T(8,128)}, u32[]{:S(2)}, u32[]{:S(2)}) collective-permute-start(f32[512,512]{1,0:T(8,128)S(1)} %shard_map.49.refs_2_), channel_id=1, source_target_pairs={{8,9},{9,8},{10,11},{11,10},{12,13},{13,12},{14,15},{15,14},{16,17... | collective-permute-start | bytes 3145736 | tf_op jit(solution)/shard_map/ppermute | solution.py:260
  194.7 1.9 collective-permute-start.13
  196.8 1.4 collective-permute-start.18
  199.6 2.4 collective-permute-start.25
  205.3 7.5 %collective-permute-done.16.refs_1_ = f32[512,512]{1,0:T(8,128)S(1)} collective-permute-done((f32[512,512]{1,0:T(8,128)S(1)}, f32[512,512]{1,0:T(8,128)S(1)}, u32[]{:S(2)}, u32[]{:S(2)}) %collective-permute-start.16) | collective-permute-done | bytes 1048608 | tf_op jit(solution)/shard_map/ppermute | solution.py:260
  213.7 19.4 %collective-permute-start.26 = (f32[512,512]{1,0:T(8,128)}, f32[512,512]{1,0:T(8,128)}, u32[]{:S(2)}, u32[]{:S(2)}) collective-permute-start(f32[512,512]{1,0:T(8,128)} %shard_map.60.refs_8_.refs_3_), channel_id=1, source_target_pairs={{16,17},{17,16},{18,19},{19,18},{20,21},{21,20},{22,23},{23,22},{2... | collective-permute-start | bytes 3145736 | tf_op jit(solution)/shard_map/ppermute | solution.py:260
  236.9 1.8 collective-permute-done.18.refs_1_
  238.7 1.7 collective-permute-start.32
  242.6 1.8 collective-permute-start.27
  248.2 1.8 shard_map.56.refs_4_
  250.0 9.3 %collective-permute-start.19 = (f32[512,512]{1,0:T(8,128)S(1)}, f32[512,512]{1,0:T(8,128)S(1)}, u32[]{:S(2)}, u32[]{:S(2)}) collective-permute-start(f32[512,512]{1,0:T(8,128)S(1)} %shard_map.54.refs_3_), channel_id=1, source_target_pairs={{24,25},{25,24},{26,27},{27,26},{28,29},{29,28},{30,31},{31,30}} | collective-permute-start | bytes 3145736 | tf_op jit(solution)/shard_map/ppermute | solution.py:260
  260.1 3.2 collective-permute-start.20
  263.3 19.2 %collective-permute-done.7.refs_1_ = f32[1024,256]{1,0:T(8,128)} collective-permute-done((f32[1024,256]{1,0:T(8,128)}, f32[1024,256]{1,0:T(8,128)}, u32[]{:S(2)}, u32[]{:S(2)}) %collective-permute-start.7) | collective-permute-done | bytes 1048608 | tf_op jit(solution)/shard_map/ppermute | solution.py:260
  285.2 1.4 shard_map.62.refs_0_
  286.6 1.4 collective-permute-start.14
  289.5 1.4 collective-permute-start.33
  294.5 14.1 %collective-permute-done.31.refs_2_ = f32[1024,256]{1,0:T(8,128)} collective-permute-done((f32[1024,256]{1,0:T(8,128)}, f32[1024,256]{1,0:T(8,128)}, u32[]{:S(2)}, u32[]{:S(2)}) %collective-permute-start.31) | collective-permute-done | bytes 1048608 | tf_op jit(solution)/shard_map/ppermute | solution.py:260
  309.8 10.5 %shard_map.68.refs_0_ = f32[1024,256]{1,0:T(8,128)S(1)} custom-call(f32[1024,256]{1,0:T(8,128)S(1)} %copy-done.19, f32[1024,256]{1,0:T(8,128)} %collective-permute-done.30.refs_1_, f32[1024,256]{1,0:T(8,128)} %collective-permute-done.31.refs_2_, f32[512,512]{1,0:T(8,128)S(1)} %copy-done.32, f32[512,512]{1,0:T(8,128)S(1)} %shard_map.56.refs_4_, ...), custom_call_target="tpu_custom_call" | custom-call | flops 4831838208 | bytes 1048576 | tf_op jit(solution)/shard_map/pallas_call | solution.py:208
  321.3 9.8 %collective-permute-done.14.refs_2_ = f32[1024,256]{1,0:T(8,128)} collective-permute-done((f32[1024,256]{1,0:T(8,128)}, f32[1024,256]{1,0:T(8,128)}, u32[]{:S(2)}, u32[]{:S(2)}) %collective-permute-start.14) | collective-permute-done | bytes 1048608 | tf_op jit(solution)/shard_map/ppermute | solution.py:260
  332.3 10.5 %shard_map.61.refs_0_ = f32[1024,256]{1,0:T(8,128)S(1)} custom-call(f32[1024,256]{1,0:T(8,128)S(1)} %copy-done.17, f32[1024,256]{1,0:T(8,128)} %collective-permute-done.7.refs_1_, f32[1024,256]{1,0:T(8,128)} %collective-permute-done.14.refs_2_, f32[512,512]{1,0:T(8,128)S(1)} %copy-done.32, f32[512,512]{1,0:T(8,128)S(1)} %shard_map.56.refs_4_, ...), custom_call_target="tpu_custom_call" | custom-call | flops 4831838208 | bytes 1048576 | tf_op jit(solution)/shard_map/pallas_call | solution.py:208
  342.9 9.1 %shard_map.71 = f32[1024,256]{1,0:T(8,128)S(1)} custom-call(f32[1024,256]{1,0:T(8,128)S(1)} %copy-done.41, f32[1024,256]{1,0:T(8,128)} %collective-permute-done.33.refs_1_, f32[512,512]{1,0:T(8,128)S(1)} %copy-done.23, f32[512,512]{1,0:T(8,128)S(1)} %copy-done.26, f32[512,512]{1,0:T(8,128)} %collective-permute-done.12.refs_4_, ...), custom_call_target="tpu_custom_call" | custom-call | flops 3221225472 | bytes 1048576 | tf_op jit(solution)/shard_map/pallas_call | solution.py:208
  352.3 9.0 %shard_map.64 = f32[1024,256]{1,0:T(8,128)S(1)} custom-call(f32[1024,256]{1,0:T(8,128)S(1)} %shard_map.61.refs_0_, f32[1024,256]{1,0:T(8,128)} %collective-permute-done.28.refs_1_, f32[512,512]{1,0:T(8,128)S(1)} %copy-done.23, f32[512,512]{1,0:T(8,128)S(1)} %copy-done.26, f32[512,512]{1,0:T(8,128)} %collective-permute-done.12.refs_4_, ...), custom_call_target="tpu_custom_call" | custom-call | flops 3221225472 | bytes 1048576 | tf_op jit(solution)/shard_map/pallas_call | solution.py:208
  361.9 4.5 %shard_map.72 = f32[2560,256]{1,0:T(8,128)S(1)} custom-call(f32[1024,512]{1,0:T(8,128)S(1)} %pad_maximum_fusion.y_ref), custom_call_target="tpu_custom_call" | custom-call | flops 1610612736 | bytes 2621440 | tf_op jit(solution)/shard_map/pallas_call | solution.py:208
  367.5 1.7 collective-permute-start.34
  369.2 3.0 collective-permute-done.34
  372.2 1.5 dynamic-slice_add_fusion
  374.9 1.3 collective-permute-start.36
  377.6 20.9 %collective-permute-done.37 = f32[320,256]{1,0:T(8,128)S(1)} collective-permute-done((f32[320,256]{1,0:T(8,128)S(1)}, f32[320,256]{1,0:T(8,128)S(1)}, u32[]{:S(2)}, u32[]{:S(2)}) %collective-permute-start.37) | collective-permute-done | bytes 327712 | tf_op jit(solution)/shard_map/ppermute | solution.py:260
  398.5 4.5 %collective-permute-done.36 = f32[320,256]{1,0:T(8,128)S(1)} collective-permute-done((f32[320,256]{1,0:T(8,128)S(1)}, f32[320,256]{1,0:T(8,128)S(1)}, u32[]{:S(2)}, u32[]{:S(2)}) %collective-permute-start.36) | collective-permute-done | bytes 327712 | tf_op jit(solution)/shard_map/ppermute | solution.py:260
  404.1 3.8 collective-permute-start.38
  409.2 10.5 %collective-permute-done.38 = f32[320,256]{1,0:T(8,128)S(1)} collective-permute-done((f32[320,256]{1,0:T(8,128)S(1)}, f32[320,256]{1,0:T(8,128)S(1)}, u32[]{:S(2)}, u32[]{:S(2)}) %collective-permute-start.38) | collective-permute-done | bytes 327712 | tf_op jit(solution)/shard_map/ppermute | solution.py:260
  419.7 1.8 collective-permute-done.39
  421.5 16.1 %collective-permute-done.40 = f32[320,256]{1,0:T(8,128)S(1)} collective-permute-done((f32[320,256]{1,0:T(8,128)S(1)}, f32[320,256]{1,0:T(8,128)S(1)}, u32[]{:S(2)}, u32[]{:S(2)}) %collective-permute-start.40) | collective-permute-done | bytes 327712 | tf_op jit(solution)/shard_map/ppermute | solution.py:260
  437.6 1.4 collective-permute-start.41
  439.3 2.4 collective-permute-done.41
  441.8 3.5 shard_map.73
  (173 shorter events, 50.9 us)
Async XLA Ops:
  3.7 2.0 collective-permute-start
  4.5 34.1 %collective-permute-start.2 = (f32[512,512]{1,0:T(8,128)}, f32[512,512]{1,0:T(8,128)S(1)}, u32[]{:S(2)}, u32[]{:S(2)}) collective-permute-start(f32[512,512]{1,0:T(8,128)} %get-tuple-element.7.own_ref), channel_id=1, source_target_pairs={{0,4},{1,5},{10,14},{11,15},{20,16},{21,17},{30,26},{31,27}} | collective-permute-start | bytes 3145736 | tf_op jit(solution)/shard_map/ppermute | solution.py:260
  7.1 35.8 %collective-permute-start.1 = (f32[512,512]{1,0:T(8,128)S(1)}, f32[512,512]{1,0:T(8,128)S(1)}, u32[]{:S(2)}, u32[]{:S(2)}) collective-permute-start(f32[512,512]{1,0:T(8,128)S(1)} %shard_map.42), channel_id=1, source_target_pairs={{0,2},{4,6},{10,8},{14,12},{16,18},{20,22},{26,24},{30,28}} | collective-permute-start | bytes 3145736 | tf_op jit(solution)/shard_map/ppermute | solution.py:260
  38.6 65.6 %collective-permute-start.3 = (f32[512,512]{1,0:T(8,128)S(1)}, f32[512,512]{1,0:T(8,128)S(1)}, u32[]{:S(2)}, u32[]{:S(2)}) collective-permute-start(f32[512,512]{1,0:T(8,128)S(1)} %shard_map.44), channel_id=1, source_target_pairs={{0,2},{1,3},{4,6},{5,7},{10,8},{11,9},{14,12},{15,13},{16,18},{17,... | collective-permute-start | bytes 3145736 | tf_op jit(solution)/shard_map/ppermute | solution.py:260
  40.0 65.1 %collective-permute-start.8 = (f32[512,512]{1,0:T(8,128)S(1)}, f32[512,512]{1,0:T(8,128)S(1)}, u32[]{:S(2)}, u32[]{:S(2)}) collective-permute-start(f32[512,512]{1,0:T(8,128)S(1)} %get-tuple-element.8.own_ref), channel_id=1, source_target_pairs={{8,12},{9,13},{18,22},{19,23},{28,24},{29,25}} | collective-permute-start | bytes 3145736 | tf_op jit(solution)/shard_map/ppermute | solution.py:260
  40.7 77.2 %collective-permute-start.10 = (f32[512,512]{1,0:T(8,128)S(1)}, f32[512,512]{1,0:T(8,128)S(1)}, u32[]{:S(2)}, u32[]{:S(2)}) collective-permute-start(f32[512,512]{1,0:T(8,128)S(1)} %get-tuple-element.9.own_ref), channel_id=1, source_target_pairs={{8,12},{9,13},{18,22},{19,23},{28,24},{29,25}} | collective-permute-start | bytes 3145736 | tf_op jit(solution)/shard_map/ppermute | solution.py:260
  41.5 76.6 %collective-permute-start.21 = (f32[512,512]{1,0:T(8,128)S(1)}, f32[512,512]{1,0:T(8,128)S(1)}, u32[]{:S(2)}, u32[]{:S(2)}) collective-permute-start(f32[512,512]{1,0:T(8,128)S(1)} %get-tuple-element.8.own_ref), channel_id=1, source_target_pairs={{16,20},{17,21},{26,30},{27,31}} | collective-permute-start | bytes 3145736 | tf_op jit(solution)/shard_map/ppermute | solution.py:260
  42.8 76.6 %collective-permute-start.23 = (f32[512,512]{1,0:T(8,128)S(1)}, f32[512,512]{1,0:T(8,128)S(1)}, u32[]{:S(2)}, u32[]{:S(2)}) collective-permute-start(f32[512,512]{1,0:T(8,128)S(1)} %get-tuple-element.9.own_ref), channel_id=1, source_target_pairs={{16,20},{17,21},{26,30},{27,31}} | collective-permute-start | bytes 3145736 | tf_op jit(solution)/shard_map/ppermute | solution.py:260
  44.3 196.1 %copy-start.2 = (f32[512,512]{1,0:T(8,128)}, f32[512,512]{1,0:T(8,128)S(1)}, u32[]{:S(2)}) copy-start(f32[512,512]{1,0:T(8,128)S(1)} %shard_map.43.refs_1_.refs_6_) | copy-start | bytes 3145732
  104.2 16.8 %collective-permute-start.15 = (f32[512,512]{1,0:T(8,128)S(1)}, f32[512,512]{1,0:T(8,128)S(1)}, u32[]{:S(2)}, u32[]{:S(2)}) collective-permute-start(f32[512,512]{1,0:T(8,128)S(1)} %get-tuple-element.8.own_ref), channel_id=1, source_target_pairs={{24,28},{25,29}} | collective-permute-start | bytes 3145736 | tf_op jit(solution)/shard_map/ppermute | solution.py:260
  105.1 135.3 %copy-start.4 = (f32[512,512]{1,0:T(8,128)}, f32[512,512]{1,0:T(8,128)S(1)}, u32[]{:S(2)}) copy-start(f32[512,512]{1,0:T(8,128)S(1)} %shard_map.45.refs_2_.refs_7_) | copy-start | bytes 3145732
  105.1 16.7 %collective-permute-start.4 = (f32[512,512]{1,0:T(8,128)S(1)}, f32[512,512]{1,0:T(8,128)S(1)}, u32[]{:S(2)}, u32[]{:S(2)}) collective-permute-start(f32[512,512]{1,0:T(8,128)S(1)} %shard_map.43.refs_1_.refs_6_), channel_id=1, source_target_pairs={{0,1},{1,0},{2,3},{3,2},{4,5},{5,4},{6,7},{7,6},{8,9},{9,8},{10,11... | collective-permute-start | bytes 3145736 | tf_op jit(solution)/shard_map/ppermute | solution.py:260
  117.9 10.3 %collective-permute-start.5 = (f32[512,512]{1,0:T(8,128)S(1)}, f32[512,512]{1,0:T(8,128)S(1)}, u32[]{:S(2)}, u32[]{:S(2)}) collective-permute-start(f32[512,512]{1,0:T(8,128)S(1)} %shard_map.45.refs_2_.refs_7_), channel_id=1, source_target_pairs={{0,1},{1,0},{2,3},{3,2},{4,5},{5,4},{6,7},{7,6},{8,9},{9,8},{10,11... | collective-permute-start | bytes 3145736 | tf_op jit(solution)/shard_map/ppermute | solution.py:260
  118.1 27.8 %collective-permute-start.9 = (f32[512,512]{1,0:T(8,128)S(1)}, f32[512,512]{1,0:T(8,128)S(1)}, u32[]{:S(2)}, u32[]{:S(2)}) collective-permute-start(f32[512,512]{1,0:T(8,128)S(1)} %shard_map.48), channel_id=1, source_target_pairs={{8,10},{9,11},{12,14},{13,15},{18,16},{19,17},{22,20},{23,21},{24,... | collective-permute-start | bytes 3145736 | tf_op jit(solution)/shard_map/ppermute | solution.py:260
  119.5 48.9 %collective-permute-start.11 = (f32[512,512]{1,0:T(8,128)S(1)}, f32[512,512]{1,0:T(8,128)S(1)}, u32[]{:S(2)}, u32[]{:S(2)}) collective-permute-start(f32[512,512]{1,0:T(8,128)S(1)} %shard_map.50), channel_id=1, source_target_pairs={{8,10},{9,11},{12,14},{13,15},{18,16},{19,17},{22,20},{23,21},{24,... | collective-permute-start | bytes 3145736 | tf_op jit(solution)/shard_map/ppermute | solution.py:260
  121.0 50.7 %collective-permute-start.17 = (f32[512,512]{1,0:T(8,128)S(1)}, f32[512,512]{1,0:T(8,128)S(1)}, u32[]{:S(2)}, u32[]{:S(2)}) collective-permute-start(f32[512,512]{1,0:T(8,128)S(1)} %get-tuple-element.9.own_ref), channel_id=1, source_target_pairs={{24,28},{25,29}} | collective-permute-start | bytes 3145736 | tf_op jit(solution)/shard_map/ppermute | solution.py:260
  121.7 118.7 %copy-start.12 = (f32[512,512]{1,0:T(8,128)}, f32[512,512]{1,0:T(8,128)S(1)}, u32[]{:S(2)}) copy-start(f32[512,512]{1,0:T(8,128)S(1)} %collective-permute-done.4.refs_3_.refs_8_) | copy-start | bytes 3145732
  121.8 51.2 %collective-permute-start.22 = (f32[512,512]{1,0:T(8,128)S(1)}, f32[512,512]{1,0:T(8,128)}, u32[]{:S(2)}, u32[]{:S(2)}) collective-permute-start(f32[512,512]{1,0:T(8,128)S(1)} %shard_map.57), channel_id=1, source_target_pairs={{16,18},{17,19},{20,22},{21,23},{26,24},{27,25},{30,28},{31,29}} | collective-permute-start | bytes 3145736 | tf_op jit(solution)/shard_map/ppermute | solution.py:260
  128.2 112.2 %copy-start.14 = (f32[512,512]{1,0:T(8,128)}, f32[512,512]{1,0:T(8,128)S(1)}, u32[]{:S(2)}) copy-start(f32[512,512]{1,0:T(8,128)S(1)} %collective-permute-done.5.refs_4_.refs_9_) | copy-start | bytes 3145732
  128.2 66.5 %collective-permute-start.24 = (f32[512,512]{1,0:T(8,128)S(1)}, f32[512,512]{1,0:T(8,128)S(1)}, u32[]{:S(2)}, u32[]{:S(2)}) collective-permute-start(f32[512,512]{1,0:T(8,128)S(1)} %shard_map.59), channel_id=1, source_target_pairs={{16,18},{17,19},{20,22},{21,23},{26,24},{27,25},{30,28},{31,29}} | collective-permute-start | bytes 3145736 | tf_op jit(solution)/shard_map/ppermute | solution.py:260
  131.3 104.5 %copy-start.18 = (f32[1024,256]{1,0:T(8,128)}, f32[1024,256]{1,0:T(8,128)S(1)}, u32[]{:S(2)}) copy-start(f32[1024,256]{1,0:T(8,128)S(1)} %get-tuple-element.13.refs_0_) | copy-start | bytes 3145732
  131.3 109.1 %copy-start.16 = (f32[1024,256]{1,0:T(8,128)}, f32[1024,256]{1,0:T(8,128)S(1)}, u32[]{:S(2)}) copy-start(f32[1024,256]{1,0:T(8,128)S(1)} %get-tuple-element.12.refs_0_) | copy-start | bytes 3145732
  145.9 50.9 %collective-permute-start.29 = (f32[1024,256]{1,0:T(8,128)S(1)}, f32[1024,256]{1,0:T(8,128)S(1)}, u32[]{:S(2)}, u32[]{:S(2)}) collective-permute-start(f32[1024,256]{1,0:T(8,128)S(1)} %shard_map.65.refs_0_), channel_id=1, source_target_pairs={{0,8},{1,9},{2,10},{3,11},{4,12},{5,13},{6,14},{7,15}} | collective-permute-start | bytes 3145736 | tf_op jit(solution)/shard_map/ppermute | solution.py:260
  169.3 30.2 %collective-permute-start.6 = (f32[1024,256]{1,0:T(8,128)S(1)}, f32[1024,256]{1,0:T(8,128)S(1)}, u32[]{:S(2)}, u32[]{:S(2)}) collective-permute-start(f32[1024,256]{1,0:T(8,128)S(1)} %shard_map.46.refs_0_), channel_id=1, source_target_pairs={{0,8},{1,9},{2,10},{3,11},{4,12},{5,13},{6,14},{7,15}} | collective-permute-start | bytes 3145736 | tf_op jit(solution)/shard_map/ppermute | solution.py:260
  171.7 41.1 %collective-permute-start.16 = (f32[512,512]{1,0:T(8,128)S(1)}, f32[512,512]{1,0:T(8,128)S(1)}, u32[]{:S(2)}, u32[]{:S(2)}) collective-permute-start(f32[512,512]{1,0:T(8,128)S(1)} %shard_map.53), channel_id=1, source_target_pairs={{24,26},{25,27},{28,30},{29,31}} | collective-permute-start | bytes 3145736 | tf_op jit(solution)/shard_map/ppermute | solution.py:260
  173.0 60.2 %collective-permute-start.12 = (f32[512,512]{1,0:T(8,128)S(1)}, f32[512,512]{1,0:T(8,128)}, u32[]{:S(2)}, u32[]{:S(2)}) collective-permute-start(f32[512,512]{1,0:T(8,128)S(1)} %shard_map.49.refs_2_), channel_id=1, source_target_pairs={{8,9},{9,8},{10,11},{11,10},{12,13},{13,12},{14,15},{15,14},{16,17... | collective-permute-start | bytes 3145736 | tf_op jit(solution)/shard_map/ppermute | solution.py:260
  194.7 39.7 %collective-permute-start.13 = (f32[512,512]{1,0:T(8,128)S(1)}, f32[512,512]{1,0:T(8,128)}, u32[]{:S(2)}, u32[]{:S(2)}) collective-permute-start(f32[512,512]{1,0:T(8,128)S(1)} %shard_map.51.refs_3_), channel_id=1, source_target_pairs={{8,9},{9,8},{10,11},{11,10},{12,13},{13,12},{14,15},{15,14},{16,17... | collective-permute-start | bytes 3145736 | tf_op jit(solution)/shard_map/ppermute | solution.py:260
  196.8 41.9 %collective-permute-start.18 = (f32[512,512]{1,0:T(8,128)S(1)}, f32[512,512]{1,0:T(8,128)}, u32[]{:S(2)}, u32[]{:S(2)}) collective-permute-start(f32[512,512]{1,0:T(8,128)S(1)} %shard_map.55), channel_id=1, source_target_pairs={{24,26},{25,27},{28,30},{29,31}} | collective-permute-start | bytes 3145736 | tf_op jit(solution)/shard_map/ppermute | solution.py:260
  199.6 43.1 %collective-permute-start.25 = (f32[512,512]{1,0:T(8,128)S(1)}, f32[512,512]{1,0:T(8,128)}, u32[]{:S(2)}, u32[]{:S(2)}) collective-permute-start(f32[512,512]{1,0:T(8,128)S(1)} %shard_map.58.refs_7_.refs_2_), channel_id=1, source_target_pairs={{16,17},{17,16},{18,19},{19,18},{20,21},{21,20},{22,23},{23,22},{2... | collective-permute-start | bytes 3145736 | tf_op jit(solution)/shard_map/ppermute | solution.py:260
  213.7 36.2 %collective-permute-start.26 = (f32[512,512]{1,0:T(8,128)}, f32[512,512]{1,0:T(8,128)}, u32[]{:S(2)}, u32[]{:S(2)}) collective-permute-start(f32[512,512]{1,0:T(8,128)} %shard_map.60.refs_8_.refs_3_), channel_id=1, source_target_pairs={{16,17},{17,16},{18,19},{19,18},{20,21},{21,20},{22,23},{23,22},{2... | collective-permute-start | bytes 3145736 | tf_op jit(solution)/shard_map/ppermute | solution.py:260
  233.2 26.9 %collective-permute-start.30 = (f32[1024,256]{1,0:T(8,128)}, f32[1024,256]{1,0:T(8,128)}, u32[]{:S(2)}, u32[]{:S(2)}) collective-permute-start(f32[1024,256]{1,0:T(8,128)} %shard_map.66), channel_id=1, source_target_pairs={{0,16},{1,17},{2,18},{3,19},{4,20},{5,21},{6,22},{7,23},{8,24},{9,... | collective-permute-start | bytes 3145736 | tf_op jit(solution)/shard_map/ppermute | solution.py:260
  234.5 48.1 %collective-permute-start.7 = (f32[1024,256]{1,0:T(8,128)}, f32[1024,256]{1,0:T(8,128)}, u32[]{:S(2)}, u32[]{:S(2)}) collective-permute-start(f32[1024,256]{1,0:T(8,128)} %shard_map.47), channel_id=1, source_target_pairs={{0,16},{1,17},{2,18},{3,19},{4,20},{5,21},{6,22},{7,23},{8,24},{9,... | collective-permute-start | bytes 3145736 | tf_op jit(solution)/shard_map/ppermute | solution.py:260
  238.7 47.8 %collective-permute-start.32 = (f32[1024,256]{1,0:T(8,128)}, f32[1024,256]{1,0:T(8,128)}, u32[]{:S(2)}, u32[]{:S(2)}) collective-permute-start(f32[1024,256]{1,0:T(8,128)} %shard_map.67), channel_id=1, source_target_pairs={{8,16},{9,17},{10,18},{11,19},{12,20},{13,21},{14,22},{15,23}} | collective-permute-start | bytes 3145736 | tf_op jit(solution)/shard_map/ppermute | solution.py:260
  242.6 46.9 %collective-permute-start.27 = (f32[1024,256]{1,0:T(8,128)}, f32[1024,256]{1,0:T(8,128)}, u32[]{:S(2)}, u32[]{:S(2)}) collective-permute-start(f32[1024,256]{1,0:T(8,128)} %shard_map.52), channel_id=1, source_target_pairs={{8,16},{9,17},{10,18},{11,19},{12,20},{13,21},{14,22},{15,23}} | collective-permute-start | bytes 3145736 | tf_op jit(solution)/shard_map/ppermute | solution.py:260
  250.0 42.3 %collective-permute-start.19 = (f32[512,512]{1,0:T(8,128)S(1)}, f32[512,512]{1,0:T(8,128)S(1)}, u32[]{:S(2)}, u32[]{:S(2)}) collective-permute-start(f32[512,512]{1,0:T(8,128)S(1)} %shard_map.54.refs_3_), channel_id=1, source_target_pairs={{24,25},{25,24},{26,27},{27,26},{28,29},{29,28},{30,31},{31,30}} | collective-permute-start | bytes 3145736 | tf_op jit(solution)/shard_map/ppermute | solution.py:260
  260.1 34.4 %collective-permute-start.20 = (f32[512,512]{1,0:T(8,128)S(1)}, f32[512,512]{1,0:T(8,128)}, u32[]{:S(2)}, u32[]{:S(2)}) collective-permute-start(f32[512,512]{1,0:T(8,128)S(1)} %shard_map.56.refs_4_), channel_id=1, source_target_pairs={{24,25},{25,24},{26,27},{27,26},{28,29},{29,28},{30,31},{31,30}} | collective-permute-start | bytes 3145736 | tf_op jit(solution)/shard_map/ppermute | solution.py:260
  282.6 26.0 %collective-permute-start.31 = (f32[1024,256]{1,0:T(8,128)}, f32[1024,256]{1,0:T(8,128)}, u32[]{:S(2)}, u32[]{:S(2)}) collective-permute-start(f32[1024,256]{1,0:T(8,128)} %shard_map.67), channel_id=1, source_target_pairs={{8,24},{9,25},{10,26},{11,27},{12,28},{13,29},{14,30},{15,31}} | collective-permute-start | bytes 3145736 | tf_op jit(solution)/shard_map/ppermute | solution.py:260
  286.6 44.5 %collective-permute-start.14 = (f32[1024,256]{1,0:T(8,128)}, f32[1024,256]{1,0:T(8,128)}, u32[]{:S(2)}, u32[]{:S(2)}) collective-permute-start(f32[1024,256]{1,0:T(8,128)} %shard_map.52), channel_id=1, source_target_pairs={{8,24},{9,25},{10,26},{11,27},{12,28},{13,29},{14,30},{15,31}} | collective-permute-start | bytes 3145736 | tf_op jit(solution)/shard_map/ppermute | solution.py:260
  289.5 53.3 %collective-permute-start.33 = (f32[1024,256]{1,0:T(8,128)S(1)}, f32[1024,256]{1,0:T(8,128)}, u32[]{:S(2)}, u32[]{:S(2)}) collective-permute-start(f32[1024,256]{1,0:T(8,128)S(1)} %shard_map.70), channel_id=1, source_target_pairs={{16,24},{17,25},{18,26},{19,27},{20,28},{21,29},{22,30},{23,31}} | collective-permute-start | bytes 3145736 | tf_op jit(solution)/shard_map/ppermute | solution.py:260
  293.2 59.1 %collective-permute-start.28 = (f32[1024,256]{1,0:T(8,128)S(1)}, f32[1024,256]{1,0:T(8,128)}, u32[]{:S(2)}, u32[]{:S(2)}) collective-permute-start(f32[1024,256]{1,0:T(8,128)S(1)} %shard_map.63), channel_id=1, source_target_pairs={{16,24},{17,25},{18,26},{19,27},{20,28},{21,29},{22,30},{23,31}} | collective-permute-start | bytes 3145736 | tf_op jit(solution)/shard_map/ppermute | solution.py:260
  367.5 4.7 %collective-permute-start.34 = (f32[1280,256]{1,0:T(8,128)}, f32[1280,256]{1,0:T(8,128)}, u32[]{:S(2)}, u32[]{:S(2)}) collective-permute-start(f32[1280,256]{1,0:T(8,128)} %constant_dynamic-slice_fusion.3), channel_id=1, source_target_pairs={{0,1},{1,0},{2,3},{3,2},{4,5},{5,4},{6,7},{7,6},{8,9},{9,8},{10,11... | collective-permute-start | bytes 3932168 | tf_op jit(solution)/shard_map/ppermute | solution.py:260
  374.9 23.6 %collective-permute-start.37 = (f32[320,256]{1,0:T(8,128)S(1)}, f32[320,256]{1,0:T(8,128)S(1)}, u32[]{:S(2)}, u32[]{:S(2)}) collective-permute-start(f32[320,256]{1,0:T(8,128)S(1)} %get-tuple-element.17), channel_id=1, source_target_pairs={{0,6},{1,7},{2,4},{3,5},{4,2},{5,3},{6,0},{7,1},{8,14},{9,15},{10,... | collective-permute-start | bytes 983048 | tf_op jit(solution)/shard_map/ppermute | solution.py:260
  374.9 28.0 %collective-permute-start.36 = (f32[320,256]{1,0:T(8,128)S(1)}, f32[320,256]{1,0:T(8,128)S(1)}, u32[]{:S(2)}, u32[]{:S(2)}) collective-permute-start(f32[320,256]{1,0:T(8,128)S(1)} %get-tuple-element.18), channel_id=1, source_target_pairs={{0,4},{1,5},{2,6},{3,7},{4,0},{5,1},{6,2},{7,3},{8,12},{9,13},{10,... | collective-permute-start | bytes 983048 | tf_op jit(solution)/shard_map/ppermute | solution.py:260
  376.3 26.7 %collective-permute-start.35 = (f32[320,256]{1,0:T(8,128)S(1)}, f32[320,256]{1,0:T(8,128)S(1)}, u32[]{:S(2)}, u32[]{:S(2)}) collective-permute-start(f32[320,256]{1,0:T(8,128)S(1)} %get-tuple-element.16), channel_id=1, source_target_pairs={{0,2},{1,3},{2,0},{3,1},{4,6},{5,7},{6,4},{7,5},{8,10},{9,11},{10,... | collective-permute-start | bytes 983048 | tf_op jit(solution)/shard_map/ppermute | solution.py:260
  404.1 15.6 %collective-permute-start.38 = (f32[320,256]{1,0:T(8,128)S(1)}, f32[320,256]{1,0:T(8,128)S(1)}, u32[]{:S(2)}, u32[]{:S(2)}) collective-permute-start(f32[320,256]{1,0:T(8,128)S(1)} %get-tuple-element.11), channel_id=1, source_target_pairs={{0,2},{1,3},{2,0},{3,1},{4,6},{5,7},{6,4},{7,5},{8,10},{9,11},{10,... | collective-permute-start | bytes 983048 | tf_op jit(solution)/shard_map/ppermute | solution.py:260
  407.9 13.6 %collective-permute-start.39 = (f32[320,256]{1,0:T(8,128)S(1)}, f32[320,256]{1,0:T(8,128)S(1)}, u32[]{:S(2)}, u32[]{:S(2)}) collective-permute-start(f32[320,256]{1,0:T(8,128)S(1)} %get-tuple-element.11), channel_id=1, source_target_pairs={{0,4},{1,5},{2,6},{3,7},{4,0},{5,1},{6,2},{7,3},{8,12},{9,13},{10,... | collective-permute-start | bytes 983048 | tf_op jit(solution)/shard_map/ppermute | solution.py:260
  407.9 29.7 %collective-permute-start.40 = (f32[320,256]{1,0:T(8,128)S(1)}, f32[320,256]{1,0:T(8,128)S(1)}, u32[]{:S(2)}, u32[]{:S(2)}) collective-permute-start(f32[320,256]{1,0:T(8,128)S(1)} %get-tuple-element.11), channel_id=1, source_target_pairs={{0,6},{1,7},{2,4},{3,5},{4,2},{5,3},{6,0},{7,1},{8,14},{9,15},{10,... | collective-permute-start | bytes 983048 | tf_op jit(solution)/shard_map/ppermute | solution.py:260
  437.6 4.1 collective-permute-start.41
  (38 other events, 494.8 us)
where the time goes:
time: 447 us; the launch traced here: 445 us
  waiting for transfers between devices  238 us (53%)
  starting transfers between devices  118 us (26%)
  Pallas kernels  65 us (15%)
  local copies, waits for them, and re-layouts  19.1 us (4%)
    ppermute x42, waiting for transfers between devices, shift(): return lax.ppermute(x, AXES, pairs)  238 us
    ppermute x42, starting transfers between devices, shift(): return lax.ppermute(x, AXES, pairs)  118 us
    pallas_call x32, Pallas kernels, call(): pl.pallas_call(kernel, out_shape=jax.ShapeDtypeStruct(out_shape, F32), in...  61.8 us
    unnamed x88, local copies, waits for them, and re-layouts  15.6 us
  transfers between devices with their start and end apart: 42, of which 17 were waited for; matrix products, arithmetic and copies ran while one was open for 1% of the time, Pallas kernels for 10%

commit v1 on v0

--- a/solution.py
+++ b/solution.py
@@ -91,6 +91,32 @@
     return call(functools.partial(pick_kernel, take_own), own.shape, [own, *got], flops=own.size)
 
 
+def gather_kernel(take_own, pieces, *refs):
+    own, got, o_ref = refs[:pieces], refs[pieces:-1], refs[-1]
+    mine = take_own(lax.axis_index("band"), lax.axis_index("ga"))
+    rows = own[0].shape[0]
+    for i in range(pieces):
+        at = pl.ds(i * rows, rows)
+
+        @pl.when(mine)
+        def _():
+            o_ref[at, :] = own[i][...]
+
+        @pl.when(jnp.logical_not(mine))
+        def _():
+            value = got[i][...]
+            for ref in got[i + pieces :: pieces]:
+                value = value + ref[...]
+            o_ref[at, :] = value
+
+
+def gathered(take_own, own, got):
+    shape = (sum(x.shape[0] for x in own), own[0].shape[1])
+    kernel = functools.partial(gather_kernel, take_own, len(own))
+    stages = len(got[0])
+    return call(kernel, shape, [*own, *(x[t] for t in range(stages) for x in got)], flops=2**20)
+
+
 def fetch(blocks, lbuf, sem, core):
     wide = lbuf.shape[2] // 2
     copies = []
@@ -231,14 +257,26 @@
     return [piece for mine, other in blocks for piece in mine + other]
 
 
-def pick_band(a, own, other):
-    return pick(lambda band, ga: band == a, own, other)
-
-
 def routes(s, nb):
     if nb == 4:
-        return {0: [[(0, 1)], [(0, 2), (1, 3)]], 1: [[(1, 2)], [(1, 3)]], 2: [[(2, 3)]]}[s]
+        return {0: [[(0, 1)], [(0, 2)], [(2, 3)]], 1: [[(1, 2)], [(1, 3)]], 2: [[(2, 3)]]}[s]
     return [[(s, b)] for b in range(s + 1, nb)]
+
+
+def tree(k, nq):
+    if nq == 4:
+        return {
+            0: [[(0, 2)], [(0, 1), (2, 3)]],
+            1: [[(1, 2)], [(1, 0), (2, 3)]],
+            2: [[(2, 3)], [(2, 0), (3, 1)]],
+            3: [[(3, 1)], [(3, 2), (1, 0)]],
+        }[k]
+    steps = []
+    bit = nq // 2
+    while bit:
+        steps.append([(q, q ^ bit) for q in range(nq) if (q ^ k) & (2 * bit - 1) == 0])
+        bit //= 2
+    return steps
 
 
 def stages(nq):
@@ -285,22 +323,20 @@
         return pick(lambda band, ga: ga // 2 == band - d, source[d][i], *got[d][i])
 
     for t in range(stages(nq)):
-        bit = nq >> (t + 1)
         for d in range(nb):
             for i in range(PIECES):
-                hops = []
-                for b in range(d, nb):
-                    for q in range(nq):
-                        if (q ^ (b - d)) & (2 * bit - 1) == 0:
-                            for c in range(2):
-                                if d or c * (n // 2) < (i + 1) * rows:
-                                    hops.append(((b, q, c), (b, q ^ bit, c)))
+                hops = [
+                    ((b, q, c), (b, to, c))
+                    for b in range(d, nb)
+                    for q, to in tree(b - d, nq)[t]
+                    for c in range(2)
+                    if d or c * (n // 2) < (i + 1) * rows
+                ]
                 got[d][i].append(shift(merged(d, i), hops))
     blocks = []
     for d in range(nb):
-        mine = [merged(d, i) for i in range(PIECES)]
-        other = [swap(x, range(d, nb)) for x in mine]
-        blocks.append((mine, other))
+        mine = gathered(lambda band, ga: ga // 2 == band - d, source[d], got[d])
+        blocks.append(([mine], [swap(mine, range(d, nb))]))
 
     wc = w // CHUNKS
     seen = [{} for _ in range(CHUNKS)]
@@ -309,7 +345,7 @@
     def apply(s, final, rhs, x, ks):
         need = [blocks[s - k] for k in ks] + ([blocks[0]] if final else [])
         return call(
-            lambda *refs: band_kernel(s, final, PIECES, len(ks), *refs),
+            lambda *refs: band_kernel(s, final, 1, len(ks), *refs),
             (n, wc),
             [rhs] + [seen[x][k, s] for k in ks],
             flat(need),
@@ -326,9 +362,7 @@
             done[x].append(solved)
             have = {s: solved}
             for hops in routes(s, nb) if s + 1 < nb else []:
-                give = None
-                for a, _ in hops:
-                    give = have[a] if give is None else pick_band(a, have[a], give)
+                give = have[hops[0][0]]
                 took = shift(
                     give,
                     [((a, q, c), (b, q, c)) for a, b in hops for q in range(nq) for c in range(2)],

time: 447 us -> 490 us (1.096)
  starting transfers between devices: 118 us -> 163 us
  local copies, waits for them, and re-layouts: 19.1 us -> 13.1 us
  waiting for transfers between devices: 238 us -> 243 us
    ppermute x42 -> x40, starting transfers between devices: 118 us -> 163 us  [shift(): return lax.ppermute(x, AXES, pairs)]
    unnamed x88 -> x44, local copies, waits for them, and re-layouts: 15.6 us -> 11 us
    ppermute x42 -> x40, waiting for transfers between devices: 238 us -> 243 us  [shift(): return lax.ppermute(x, AXES, pairs)]
    pallas_call x32 -> x26, Pallas kernels: 61.8 us -> 58.9 us  [call(): pl.pallas_call(kernel, out_shape=jax.ShapeDtypeStruct(out_shape, F32), in...]
  transfers between devices with their start and end apart: 42 -> 40, of which waited for: 17 -> 16; matrix products, arithmetic and copies ran while one was open for 1% -> 0% of each run, Pallas kernels for 10% -> 9%
where the time goes in v1:
time: 490 us; the launch traced here: 488 us
  waiting for transfers between devices  243 us (50%)
  starting transfers between devices  163 us (33%)
  Pallas kernels  62.1 us (13%)
  local copies, waits for them, and re-layouts  13.1 us (3%)
  other arithmetic  5.87 us (1%)
    ppermute x40, waiting for transfers between devices, shift(): return lax.ppermute(x, AXES, pairs)  243 us
    ppermute x40, starting transfers between devices, shift(): return lax.ppermute(x, AXES, pairs)  163 us
    pallas_call x26, Pallas kernels, call(): pl.pallas_call(kernel, out_shape=jax.ShapeDtypeStruct(out_shape, F32), in...  58.9 us
    unnamed x44, local copies, waits for them, and re-layouts  11 us
  transfers between devices with their start and end apart: 40, of which 16 were waited for; matrix products, arithmetic and copies ran while one was open for 0% of the time, Pallas kernels for 9%

profile of v1, /device:TPU:15, one launch (start us, length us, event | category | flops | bytes accessed | tf_op | source)
XLA Modules:
  0.0 488.2 jit_solution(18010062251373005880)
XLA Ops:
  0.6 3.3 shard_map.41
  4.6 1.4 collective-permute-start.1
  8.7 30.2 %collective-permute-done.1.refs_0_.refs_3_ = f32[512,512]{1,0:T(8,128)S(1)} collective-permute-done((f32[512,512]{1,0:T(8,128)}, f32[512,512]{1,0:T(8,128)S(1)}, u32[]{:S(2)}, u32[]{:S(2)}) %collective-permute-start.1) | collective-permute-done | bytes 1048608 | tf_op jit(solution)/shard_map/ppermute | solution.py:298
  45.9 16.8 %collective-permute-done.3.refs_5_ = f32[512,512]{1,0:T(8,128)S(1)} collective-permute-done((f32[512,512]{1,0:T(8,128)S(1)}, f32[512,512]{1,0:T(8,128)S(1)}, u32[]{:S(2)}, u32[]{:S(2)}) %collective-permute-start.3) | collective-permute-done | bytes 1048608 | tf_op jit(solution)/shard_map/ppermute | solution.py:298
  63.0 25.6 %collective-permute-start.4 = (f32[1024,512]{1,0:T(8,128)S(1)}, f32[1024,512]{1,0:T(8,128)S(1)}, u32[]{:S(2)}, u32[]{:S(2)}) collective-permute-start(f32[1024,512]{1,0:T(8,128)S(1)} %shard_map.44.refs_1_.refs_4_), channel_id=1, source_target_pairs={{0,1},{1,0},{2,3},{3,2},{4,5},{5,4},{6,7},{7,6},{8,9},{9,8},{10,11... | collective-permute-start | bytes 6291464 | tf_op jit(solution)/shard_map/ppermute | solution.py:298
  90.2 42.1 %collective-permute-start.21 = (f32[512,512]{1,0:T(8,128)S(1)}, f32[512,512]{1,0:T(8,128)S(1)}, u32[]{:S(2)}, u32[]{:S(2)}) collective-permute-start(f32[512,512]{1,0:T(8,128)S(1)} %shard_map.53), channel_id=1, source_target_pairs={{16,18},{17,19},{20,22},{21,23},{26,24},{27,25},{28,30},{29,31}} | collective-permute-start | bytes 3145736 | tf_op jit(solution)/shard_map/ppermute | solution.py:298
  133.4 22.4 %collective-permute-start.22 = (f32[512,512]{1,0:T(8,128)S(1)}, f32[512,512]{1,0:T(8,128)S(1)}, u32[]{:S(2)}, u32[]{:S(2)}) collective-permute-start(f32[512,512]{1,0:T(8,128)S(1)} %shard_map.54), channel_id=1, source_target_pairs={{16,18},{17,19},{20,22},{21,23},{26,24},{27,25},{28,30},{29,31}} | collective-permute-start | bytes 3145736 | tf_op jit(solution)/shard_map/ppermute | solution.py:298
  157.3 4.7 collective-permute-start.12
  162.1 1.4 collective-permute-start.16
  163.7 11.4 %collective-permute-done.21.refs_4_ = f32[512,512]{1,0:T(8,128)S(1)} collective-permute-done((f32[512,512]{1,0:T(8,128)S(1)}, f32[512,512]{1,0:T(8,128)S(1)}, u32[]{:S(2)}, u32[]{:S(2)}) %collective-permute-start.21) | collective-permute-done | bytes 1048608 | tf_op jit(solution)/shard_map/ppermute | solution.py:298
  176.6 21.0 %collective-permute-done.22.refs_5_ = f32[512,512]{1,0:T(8,128)S(1)} collective-permute-done((f32[512,512]{1,0:T(8,128)S(1)}, f32[512,512]{1,0:T(8,128)S(1)}, u32[]{:S(2)}, u32[]{:S(2)}) %collective-permute-start.22) | collective-permute-done | bytes 1048608 | tf_op jit(solution)/shard_map/ppermute | solution.py:298
  197.7 2.4 collective-permute-start.23
  202.0 9.4 %collective-permute-done.17.refs_5_ = f32[512,512]{1,0:T(8,128)} collective-permute-done((f32[512,512]{1,0:T(8,128)S(1)}, f32[512,512]{1,0:T(8,128)}, u32[]{:S(2)}, u32[]{:S(2)}) %collective-permute-start.17) | collective-permute-done | bytes 1048608 | tf_op jit(solution)/shard_map/ppermute | solution.py:298
  211.4 2.8 shard_map.52.refs_3_
  214.2 2.8 collective-permute-start.18
  218.7 1.7 collective-permute-start.26
  220.4 1.6 collective-permute-start.5
  223.1 1.6 collective-permute-start.30
  225.8 1.6 collective-permute-start.24
  228.7 1.5 collective-permute-start.27
  231.4 1.6 copy-done.11
  236.3 1.4 collective-permute-start.13
  240.4 1.4 collective-permute-start.31
  243.0 64.1 %collective-permute-done.27.refs_1_ = f32[1024,256]{1,0:T(8,128)S(1)} collective-permute-done((f32[1024,256]{1,0:T(8,128)}, f32[1024,256]{1,0:T(8,128)S(1)}, u32[]{:S(2)}, u32[]{:S(2)}) %collective-permute-start.27) | collective-permute-done | bytes 1048608 | tf_op jit(solution)/shard_map/ppermute | solution.py:298
  310.6 9.1 %shard_map.62.refs_0_ = f32[1024,256]{1,0:T(8,128)S(1)} custom-call(f32[1024,256]{1,0:T(8,128)S(1)} %copy-done.4, f32[1024,256]{1,0:T(8,128)S(1)} %copy-done.18, f32[1024,256]{1,0:T(8,128)S(1)} %collective-permute-done.29.refs_2_, f32[1024,512]{1,0:T(8,128)} %shard_map.52.refs_3_, f32[1024,512]{1,0:T(8,128)} %collective-permute-done.18.refs_4_, ...), custom_call_target="tpu_custom_call" | custom-call | flops 4831838208 | bytes 1048576 | tf_op jit(solution)/shard_map/pallas_call | solution.py:234
  319.7 10.0 %collective-permute-done.6.refs_1_ = f32[1024,256]{1,0:T(8,128)} collective-permute-done((f32[1024,256]{1,0:T(8,128)}, f32[1024,256]{1,0:T(8,128)}, u32[]{:S(2)}, u32[]{:S(2)}) %collective-permute-start.6) | collective-permute-done | bytes 1048608 | tf_op jit(solution)/shard_map/ppermute | solution.py:298
  331.9 10.3 %shard_map.56.refs_0_ = f32[1024,256]{1,0:T(8,128)S(1)} custom-call(f32[1024,256]{1,0:T(8,128)S(1)} %get-tuple-element.12.refs_0_, f32[1024,256]{1,0:T(8,128)} %collective-permute-done.6.refs_1_, f32[1024,256]{1,0:T(8,128)S(1)} %copy-done.16, f32[1024,512]{1,0:T(8,128)} %shard_map.52.refs_3_, f32[1024,512]{1,0:T(8,128)} %collective-permute-done.18.refs_4_, ...), custom_call_target="tpu_custom_call" | custom-call | flops 4831838208 | bytes 1048576 | tf_op jit(solution)/shard_map/pallas_call | solution.py:234
  342.2 10.0 %collective-permute-done.31.refs_1_ = f32[1024,256]{1,0:T(8,128)} collective-permute-done((f32[1024,256]{1,0:T(8,128)S(1)}, f32[1024,256]{1,0:T(8,128)}, u32[]{:S(2)}, u32[]{:S(2)}) %collective-permute-start.31) | collective-permute-done | bytes 1048608 | tf_op jit(solution)/shard_map/ppermute | solution.py:298
  352.2 9.0 %shard_map.65 = f32[1024,256]{1,0:T(8,128)S(1)} custom-call(f32[1024,256]{1,0:T(8,128)S(1)} %shard_map.62.refs_0_, f32[1024,256]{1,0:T(8,128)} %collective-permute-done.31.refs_1_, f32[1024,512]{1,0:T(8,128)S(1)} %copy-done.9, f32[1024,512]{1,0:T(8,128)} %collective-permute-done.12.refs_3_, f32[1024,512]{1,0:T(8,128)S(1)} %shard_map.44.refs_1_.refs_4_, ...), custom_call_target="tpu_custom_call" | custom-call | flops 3221225472 | bytes 1048576 | tf_op jit(solution)/shard_map/pallas_call | solution.py:234
  361.2 1.5 select_select_fusion
  362.7 11.9 %collective-permute-done.25.refs_1_ = f32[1024,256]{1,0:T(8,128)} collective-permute-done((f32[1024,256]{1,0:T(8,128)S(1)}, f32[1024,256]{1,0:T(8,128)}, u32[]{:S(2)}, u32[]{:S(2)}) %collective-permute-start.25) | collective-permute-done | bytes 1048608 | tf_op jit(solution)/shard_map/ppermute | solution.py:298
  374.7 9.0 %shard_map.59 = f32[1024,256]{1,0:T(8,128)S(1)} custom-call(f32[1024,256]{1,0:T(8,128)S(1)} %shard_map.56.refs_0_, f32[1024,256]{1,0:T(8,128)} %collective-permute-done.25.refs_1_, f32[1024,512]{1,0:T(8,128)S(1)} %copy-done.9, f32[1024,512]{1,0:T(8,128)} %collective-permute-done.12.refs_3_, f32[1024,512]{1,0:T(8,128)S(1)} %shard_map.44.refs_1_.refs_4_, ...), custom_call_target="tpu_custom_call" | custom-call | flops 3221225472 | bytes 1048576 | tf_op jit(solution)/shard_map/pallas_call | solution.py:234
  383.7 1.5 select_select_fusion.1
  385.5 4.5 shard_map.66
  391.2 1.4 collective-permute-start.32
  392.6 3.0 collective-permute-done.32
  395.6 1.5 dynamic-slice_add_fusion
  398.2 21.4 %collective-permute-start.35 = (f32[320,256]{1,0:T(8,128)S(1)}, f32[320,256]{1,0:T(8,128)S(1)}, u32[]{:S(2)}, u32[]{:S(2)}) collective-permute-start(f32[320,256]{1,0:T(8,128)S(1)} %get-tuple-element.17), channel_id=1, source_target_pairs={{0,6},{1,7},{2,4},{3,5},{4,2},{5,3},{6,0},{7,1},{8,14},{9,15},{10,... | collective-permute-start | bytes 983048 | tf_op jit(solution)/shard_map/ppermute | solution.py:298
  419.6 2.0 collective-permute-start.34
  422.7 18.7 %collective-permute-done.35 = f32[320,256]{1,0:T(8,128)S(1)} collective-permute-done((f32[320,256]{1,0:T(8,128)S(1)}, f32[320,256]{1,0:T(8,128)S(1)}, u32[]{:S(2)}, u32[]{:S(2)}) %collective-permute-start.35) | collective-permute-done | bytes 327712 | tf_op jit(solution)/shard_map/ppermute | solution.py:298
  441.4 6.0 %collective-permute-done.34 = f32[320,256]{1,0:T(8,128)S(1)} collective-permute-done((f32[320,256]{1,0:T(8,128)S(1)}, f32[320,256]{1,0:T(8,128)S(1)}, u32[]{:S(2)}, u32[]{:S(2)}) %collective-permute-start.34) | collective-permute-done | bytes 327712 | tf_op jit(solution)/shard_map/ppermute | solution.py:298
  448.6 2.3 collective-permute-start.36
  452.1 11.3 %collective-permute-done.36 = f32[320,256]{1,0:T(8,128)S(1)} collective-permute-done((f32[320,256]{1,0:T(8,128)S(1)}, f32[320,256]{1,0:T(8,128)S(1)}, u32[]{:S(2)}, u32[]{:S(2)}) %collective-permute-start.36) | collective-permute-done | bytes 327712 | tf_op jit(solution)/shard_map/ppermute | solution.py:298
  463.4 2.3 collective-permute-done.37
  465.7 14.2 %collective-permute-done.38 = f32[320,256]{1,0:T(8,128)S(1)} collective-permute-done((f32[320,256]{1,0:T(8,128)S(1)}, f32[320,256]{1,0:T(8,128)S(1)}, u32[]{:S(2)}, u32[]{:S(2)}) %collective-permute-start.38) | collective-permute-done | bytes 327712 | tf_op jit(solution)/shard_map/ppermute | solution.py:298
  479.9 2.0 collective-permute-start.39
  482.2 2.4 collective-permute-done.39
  484.7 3.5 shard_map.67
  (119 shorter events, 43.6 us)
Async XLA Ops:
  0.6 5.4 %copy-start.19 = (f32[1024,512]{1,0:T(8,128)S(1)}, f32[1024,512]{1,0:T(8,128)}, u32[]{:S(2)}) copy-start(f32[1024,512]{1,0:T(8,128)} %l_ref.1) | copy-start | bytes 6291460
  3.9 4.0 collective-permute-start
  4.6 34.3 %collective-permute-start.1 = (f32[512,512]{1,0:T(8,128)}, f32[512,512]{1,0:T(8,128)S(1)}, u32[]{:S(2)}, u32[]{:S(2)}) collective-permute-start(f32[512,512]{1,0:T(8,128)} %get-tuple-element.7.own_ref.refs_1_), channel_id=1, source_target_pairs={{0,4},{1,5},{10,12},{11,13},{20,22},{21,23},{30,26},{31,27}} | collective-permute-start | bytes 3145736 | tf_op jit(solution)/shard_map/ppermute | solution.py:298
  6.3 32.7 %copy-start.6 = (f32[512,512]{1,0:T(8,128)S(1)}, f32[512,512]{1,0:T(8,128)}, u32[]{:S(2)}) copy-start(f32[512,512]{1,0:T(8,128)} %get-tuple-element.7.own_ref.refs_1_) | copy-start | bytes 3145732
  6.3 35.5 %collective-permute-start.8 = (f32[512,512]{1,0:T(8,128)S(1)}, f32[512,512]{1,0:T(8,128)S(1)}, u32[]{:S(2)}, u32[]{:S(2)}) collective-permute-start(f32[512,512]{1,0:T(8,128)S(1)} %get-tuple-element.8.own_ref.refs_0_), channel_id=1, source_target_pairs={{8,12},{9,13},{18,20},{19,21},{28,30},{29,31}} | collective-permute-start | bytes 3145736 | tf_op jit(solution)/shard_map/ppermute | solution.py:298
  7.1 36.1 %collective-permute-start.9 = (f32[512,512]{1,0:T(8,128)S(1)}, f32[512,512]{1,0:T(8,128)S(1)}, u32[]{:S(2)}, u32[]{:S(2)}) collective-permute-start(f32[512,512]{1,0:T(8,128)S(1)} %get-tuple-element.9.own_ref.refs_1_), channel_id=1, source_target_pairs={{8,12},{9,13},{18,20},{19,21},{28,30},{29,31}} | collective-permute-start | bytes 3145736 | tf_op jit(solution)/shard_map/ppermute | solution.py:298
  8.0 36.6 %collective-permute-start.2 = (f32[512,512]{1,0:T(8,128)S(1)}, f32[512,512]{1,0:T(8,128)S(1)}, u32[]{:S(2)}, u32[]{:S(2)}) collective-permute-start(f32[512,512]{1,0:T(8,128)S(1)} %shard_map.42), channel_id=1, source_target_pairs={{0,2},{4,6},{10,8},{12,14},{20,16},{22,18},{30,28},{26,24}} | collective-permute-start | bytes 3145736 | tf_op jit(solution)/shard_map/ppermute | solution.py:298
  39.0 23.7 %collective-permute-start.3 = (f32[512,512]{1,0:T(8,128)S(1)}, f32[512,512]{1,0:T(8,128)S(1)}, u32[]{:S(2)}, u32[]{:S(2)}) collective-permute-start(f32[512,512]{1,0:T(8,128)S(1)} %shard_map.43), channel_id=1, source_target_pairs={{0,2},{1,3},{4,6},{5,7},{10,8},{11,9},{12,14},{13,15},{20,16},{21,... | collective-permute-start | bytes 3145736 | tf_op jit(solution)/shard_map/ppermute | solution.py:298
  40.4 48.2 %collective-permute-start.19 = (f32[512,512]{1,0:T(8,128)S(1)}, f32[512,512]{1,0:T(8,128)S(1)}, u32[]{:S(2)}, u32[]{:S(2)}) collective-permute-start(f32[512,512]{1,0:T(8,128)S(1)} %get-tuple-element.8.own_ref.refs_0_), channel_id=1, source_target_pairs={{16,20},{17,21},{26,28},{27,29}} | collective-permute-start | bytes 3145736 | tf_op jit(solution)/shard_map/ppermute | solution.py:298
  41.7 47.6 %collective-permute-start.20 = (f32[512,512]{1,0:T(8,128)S(1)}, f32[512,512]{1,0:T(8,128)S(1)}, u32[]{:S(2)}, u32[]{:S(2)}) collective-permute-start(f32[512,512]{1,0:T(8,128)S(1)} %get-tuple-element.9.own_ref.refs_1_), channel_id=1, source_target_pairs={{16,20},{17,21},{26,28},{27,29}} | collective-permute-start | bytes 3145736 | tf_op jit(solution)/shard_map/ppermute | solution.py:298
  43.2 46.9 %collective-permute-start.10 = (f32[512,512]{1,0:T(8,128)S(1)}, f32[512,512]{1,0:T(8,128)S(1)}, u32[]{:S(2)}, u32[]{:S(2)}) collective-permute-start(f32[512,512]{1,0:T(8,128)S(1)} %shard_map.46), channel_id=1, source_target_pairs={{8,10},{9,11},{12,14},{13,15},{18,16},{19,17},{20,22},{21,23},{28,... | collective-permute-start | bytes 3145736 | tf_op jit(solution)/shard_map/ppermute | solution.py:298
  44.6 87.8 %collective-permute-start.11 = (f32[512,512]{1,0:T(8,128)S(1)}, f32[512,512]{1,0:T(8,128)S(1)}, u32[]{:S(2)}, u32[]{:S(2)}) collective-permute-start(f32[512,512]{1,0:T(8,128)S(1)} %shard_map.47), channel_id=1, source_target_pairs={{8,10},{9,11},{12,14},{13,15},{18,16},{19,17},{20,22},{21,23},{28,... | collective-permute-start | bytes 3145736 | tf_op jit(solution)/shard_map/ppermute | solution.py:298
  63.0 137.2 %collective-permute-start.4 = (f32[1024,512]{1,0:T(8,128)S(1)}, f32[1024,512]{1,0:T(8,128)S(1)}, u32[]{:S(2)}, u32[]{:S(2)}) collective-permute-start(f32[1024,512]{1,0:T(8,128)S(1)} %shard_map.44.refs_1_.refs_4_), channel_id=1, source_target_pairs={{0,1},{1,0},{2,3},{3,2},{4,5},{5,4},{6,7},{7,6},{8,9},{9,8},{10,11... | collective-permute-start | bytes 6291464 | tf_op jit(solution)/shard_map/ppermute | solution.py:298
  88.6 68.7 %collective-permute-start.14 = (f32[512,512]{1,0:T(8,128)S(1)}, f32[512,512]{1,0:T(8,128)S(1)}, u32[]{:S(2)}, u32[]{:S(2)}) collective-permute-start(f32[512,512]{1,0:T(8,128)S(1)} %get-tuple-element.8.own_ref.refs_0_), channel_id=1, source_target_pairs={{24,28},{25,29}} | collective-permute-start | bytes 3145736 | tf_op jit(solution)/shard_map/ppermute | solution.py:298
  89.3 72.8 %collective-permute-start.15 = (f32[512,512]{1,0:T(8,128)S(1)}, f32[512,512]{1,0:T(8,128)S(1)}, u32[]{:S(2)}, u32[]{:S(2)}) collective-permute-start(f32[512,512]{1,0:T(8,128)S(1)} %get-tuple-element.9.own_ref.refs_1_), channel_id=1, source_target_pairs={{24,28},{25,29}} | collective-permute-start | bytes 3145736 | tf_op jit(solution)/shard_map/ppermute | solution.py:298
  90.2 84.9 %collective-permute-start.21 = (f32[512,512]{1,0:T(8,128)S(1)}, f32[512,512]{1,0:T(8,128)S(1)}, u32[]{:S(2)}, u32[]{:S(2)}) collective-permute-start(f32[512,512]{1,0:T(8,128)S(1)} %shard_map.53), channel_id=1, source_target_pairs={{16,18},{17,19},{20,22},{21,23},{26,24},{27,25},{28,30},{29,31}} | collective-permute-start | bytes 3145736 | tf_op jit(solution)/shard_map/ppermute | solution.py:298
  133.4 64.2 %collective-permute-start.22 = (f32[512,512]{1,0:T(8,128)S(1)}, f32[512,512]{1,0:T(8,128)S(1)}, u32[]{:S(2)}, u32[]{:S(2)}) collective-permute-start(f32[512,512]{1,0:T(8,128)S(1)} %shard_map.54), channel_id=1, source_target_pairs={{16,18},{17,19},{20,22},{21,23},{26,24},{27,25},{28,30},{29,31}} | collective-permute-start | bytes 3145736 | tf_op jit(solution)/shard_map/ppermute | solution.py:298
  157.3 67.5 %copy-start.8 = (f32[1024,512]{1,0:T(8,128)}, f32[1024,512]{1,0:T(8,128)S(1)}, u32[]{:S(2)}) copy-start(f32[1024,512]{1,0:T(8,128)S(1)} %shard_map.48.refs_2_) | copy-start | bytes 6291460
  157.3 61.4 %collective-permute-start.12 = (f32[1024,512]{1,0:T(8,128)S(1)}, f32[1024,512]{1,0:T(8,128)}, u32[]{:S(2)}, u32[]{:S(2)}) collective-permute-start(f32[1024,512]{1,0:T(8,128)S(1)} %shard_map.48.refs_2_), channel_id=1, source_target_pairs={{8,9},{9,8},{10,11},{11,10},{12,13},{13,12},{14,15},{15,14},{16,17... | collective-permute-start | bytes 6291464 | tf_op jit(solution)/shard_map/ppermute | solution.py:298
  162.1 14.3 %copy-start.21 = (f32[1024,512]{1,0:T(8,128)S(1)}, f32[1024,512]{1,0:T(8,128)}, u32[]{:S(2)}) copy-start(f32[1024,512]{1,0:T(8,128)} %param.2) | copy-start | bytes 6291460
  162.1 39.9 %collective-permute-start.16 = (f32[512,512]{1,0:T(8,128)S(1)}, f32[512,512]{1,0:T(8,128)S(1)}, u32[]{:S(2)}, u32[]{:S(2)}) collective-permute-start(f32[512,512]{1,0:T(8,128)S(1)} %shard_map.50), channel_id=1, source_target_pairs={{24,26},{25,27},{28,30},{29,31}} | collective-permute-start | bytes 3145736 | tf_op jit(solution)/shard_map/ppermute | solution.py:298
  175.1 36.3 %collective-permute-start.17 = (f32[512,512]{1,0:T(8,128)S(1)}, f32[512,512]{1,0:T(8,128)}, u32[]{:S(2)}, u32[]{:S(2)}) collective-permute-start(f32[512,512]{1,0:T(8,128)S(1)} %shard_map.51), channel_id=1, source_target_pairs={{24,26},{25,27},{28,30},{29,31}} | collective-permute-start | bytes 3145736 | tf_op jit(solution)/shard_map/ppermute | solution.py:298
  176.5 45.5 %copy-start.2 = (f32[1024,256]{1,0:T(8,128)}, f32[1024,256]{1,0:T(8,128)S(1)}, u32[]{:S(2)}) copy-start(f32[1024,256]{1,0:T(8,128)S(1)} %get-tuple-element.13.refs_0_) | copy-start | bytes 3145732
  197.7 28.0 %collective-permute-start.23 = (f32[1024,512]{1,0:T(8,128)S(1)}, f32[1024,512]{1,0:T(8,128)}, u32[]{:S(2)}, u32[]{:S(2)}) collective-permute-start(f32[1024,512]{1,0:T(8,128)S(1)} %shard_map.55.refs_5_.refs_2_), channel_id=1, source_target_pairs={{16,17},{17,16},{18,19},{19,18},{20,21},{21,20},{22,23},{23,22},{2... | collective-permute-start | bytes 6291464 | tf_op jit(solution)/shard_map/ppermute | solution.py:298
  200.1 24.6 %copy-start = (f32[1024,512]{1,0:T(8,128)}, f32[1024,512]{1,0:T(8,128)S(1)}, u32[]{:S(2)}) copy-start(f32[1024,512]{1,0:T(8,128)S(1)} %collective-permute-done.4.refs_2_.refs_5_) | copy-start | bytes 6291460
  201.3 19.1 %collective-permute-start.28 = (f32[1024,256]{1,0:T(8,128)}, f32[1024,256]{1,0:T(8,128)S(1)}, u32[]{:S(2)}, u32[]{:S(2)}) collective-permute-start(f32[1024,256]{1,0:T(8,128)} %shard_map.60), channel_id=1, source_target_pairs={{0,8},{1,9},{2,10},{3,11},{4,12},{5,13},{6,14},{7,15}} | collective-permute-start | bytes 3145736 | tf_op jit(solution)/shard_map/ppermute | solution.py:298
  214.2 22.1 %collective-permute-start.18 = (f32[1024,512]{1,0:T(8,128)}, f32[1024,512]{1,0:T(8,128)}, u32[]{:S(2)}, u32[]{:S(2)}) collective-permute-start(f32[1024,512]{1,0:T(8,128)} %shard_map.52.refs_3_), channel_id=1, source_target_pairs={{24,25},{25,24},{26,27},{27,26},{28,29},{29,28},{30,31},{31,30}} | collective-permute-start | bytes 6291464 | tf_op jit(solution)/shard_map/ppermute | solution.py:298
  218.0 5.1 %collective-permute-start.7 = (f32[1024,256]{1,0:T(8,128)}, f32[1024,256]{1,0:T(8,128)S(1)}, u32[]{:S(2)}, u32[]{:S(2)}) collective-permute-start(f32[1024,256]{1,0:T(8,128)} %shard_map.45), channel_id=1, source_target_pairs={{0,8},{1,9},{2,10},{3,11},{4,12},{5,13},{6,14},{7,15}} | collective-permute-start | bytes 3145736 | tf_op jit(solution)/shard_map/ppermute | solution.py:298
  218.7 8.7 %collective-permute-start.26 = (f32[1024,256]{1,0:T(8,128)}, f32[1024,256]{1,0:T(8,128)}, u32[]{:S(2)}, u32[]{:S(2)}) collective-permute-start(f32[1024,256]{1,0:T(8,128)} %shard_map.60), channel_id=1, source_target_pairs={{0,16},{1,17},{2,18},{3,19},{4,20},{5,21},{6,22},{7,23}} | collective-permute-start | bytes 3145736 | tf_op jit(solution)/shard_map/ppermute | solution.py:298
  220.4 8.3 %collective-permute-start.5 = (f32[1024,256]{1,0:T(8,128)}, f32[1024,256]{1,0:T(8,128)}, u32[]{:S(2)}, u32[]{:S(2)}) collective-permute-start(f32[1024,256]{1,0:T(8,128)} %shard_map.45), channel_id=1, source_target_pairs={{0,16},{1,17},{2,18},{3,19},{4,20},{5,21},{6,22},{7,23}} | collective-permute-start | bytes 3145736 | tf_op jit(solution)/shard_map/ppermute | solution.py:298
  223.1 14.7 %collective-permute-start.30 = (f32[1024,256]{1,0:T(8,128)}, f32[1024,256]{1,0:T(8,128)}, u32[]{:S(2)}, u32[]{:S(2)}) collective-permute-start(f32[1024,256]{1,0:T(8,128)} %shard_map.61), channel_id=1, source_target_pairs={{8,16},{9,17},{10,18},{11,19},{12,20},{13,21},{14,22},{15,23}} | collective-permute-start | bytes 3145736 | tf_op jit(solution)/shard_map/ppermute | solution.py:298
  225.8 14.6 %collective-permute-start.24 = (f32[1024,256]{1,0:T(8,128)}, f32[1024,256]{1,0:T(8,128)}, u32[]{:S(2)}, u32[]{:S(2)}) collective-permute-start(f32[1024,256]{1,0:T(8,128)} %shard_map.49), channel_id=1, source_target_pairs={{8,16},{9,17},{10,18},{11,19},{12,20},{13,21},{14,22},{15,23}} | collective-permute-start | bytes 3145736 | tf_op jit(solution)/shard_map/ppermute | solution.py:298
  227.4 82.0 %collective-permute-start.29 = (f32[1024,256]{1,0:T(8,128)}, f32[1024,256]{1,0:T(8,128)S(1)}, u32[]{:S(2)}, u32[]{:S(2)}) collective-permute-start(f32[1024,256]{1,0:T(8,128)} %shard_map.61), channel_id=1, source_target_pairs={{8,24},{9,25},{10,26},{11,27},{12,28},{13,29},{14,30},{15,31}} | collective-permute-start | bytes 3145736 | tf_op jit(solution)/shard_map/ppermute | solution.py:298
  228.7 78.4 %collective-permute-start.27 = (f32[1024,256]{1,0:T(8,128)}, f32[1024,256]{1,0:T(8,128)S(1)}, u32[]{:S(2)}, u32[]{:S(2)}) collective-permute-start(f32[1024,256]{1,0:T(8,128)} %collective-permute-done.26.refs_1_), channel_id=1, source_target_pairs={{16,24},{17,25},{18,26},{19,27},{20,28},{21,29},{22,30},{23,31}} | collective-permute-start | bytes 3145736 | tf_op jit(solution)/shard_map/ppermute | solution.py:298
  236.3 93.4 %collective-permute-start.13 = (f32[1024,256]{1,0:T(8,128)}, f32[1024,256]{1,0:T(8,128)S(1)}, u32[]{:S(2)}, u32[]{:S(2)}) collective-permute-start(f32[1024,256]{1,0:T(8,128)} %shard_map.49), channel_id=1, source_target_pairs={{8,24},{9,25},{10,26},{11,27},{12,28},{13,29},{14,30},{15,31}} | collective-permute-start | bytes 3145736 | tf_op jit(solution)/shard_map/ppermute | solution.py:298
  237.8 92.0 %collective-permute-start.6 = (f32[1024,256]{1,0:T(8,128)}, f32[1024,256]{1,0:T(8,128)}, u32[]{:S(2)}, u32[]{:S(2)}) collective-permute-start(f32[1024,256]{1,0:T(8,128)} %collective-permute-done.5.refs_1_), channel_id=1, source_target_pairs={{16,24},{17,25},{18,26},{19,27},{20,28},{21,29},{22,30},{23,31}} | collective-permute-start | bytes 3145736 | tf_op jit(solution)/shard_map/ppermute | solution.py:298
  240.3 69.1 %copy-start.4 = (f32[1024,256]{1,0:T(8,128)S(1)}, f32[1024,256]{1,0:T(8,128)}, u32[]{:S(2)}) copy-start(f32[1024,256]{1,0:T(8,128)} %copy-done.2) | copy-start | bytes 3145732
  240.4 111.8 %collective-permute-start.31 = (f32[1024,256]{1,0:T(8,128)S(1)}, f32[1024,256]{1,0:T(8,128)}, u32[]{:S(2)}, u32[]{:S(2)}) collective-permute-start(f32[1024,256]{1,0:T(8,128)S(1)} %shard_map.64), channel_id=1, source_target_pairs={{16,24},{17,25},{18,26},{19,27},{20,28},{21,29},{22,30},{23,31}} | collective-permute-start | bytes 3145736 | tf_op jit(solution)/shard_map/ppermute | solution.py:298
  308.1 66.5 %collective-permute-start.25 = (f32[1024,256]{1,0:T(8,128)S(1)}, f32[1024,256]{1,0:T(8,128)}, u32[]{:S(2)}, u32[]{:S(2)}) collective-permute-start(f32[1024,256]{1,0:T(8,128)S(1)} %shard_map.58), channel_id=1, source_target_pairs={{16,24},{17,25},{18,26},{19,27},{20,28},{21,29},{22,30},{23,31}} | collective-permute-start | bytes 3145736 | tf_op jit(solution)/shard_map/ppermute | solution.py:298
  385.5 4.5 copy-start.7
  391.2 4.5 collective-permute-start.32
  398.2 43.2 %collective-permute-start.35 = (f32[320,256]{1,0:T(8,128)S(1)}, f32[320,256]{1,0:T(8,128)S(1)}, u32[]{:S(2)}, u32[]{:S(2)}) collective-permute-start(f32[320,256]{1,0:T(8,128)S(1)} %get-tuple-element.17), channel_id=1, source_target_pairs={{0,6},{1,7},{2,4},{3,5},{4,2},{5,3},{6,0},{7,1},{8,14},{9,15},{10,... | collective-permute-start | bytes 983048 | tf_op jit(solution)/shard_map/ppermute | solution.py:298
  419.6 27.8 %collective-permute-start.34 = (f32[320,256]{1,0:T(8,128)S(1)}, f32[320,256]{1,0:T(8,128)S(1)}, u32[]{:S(2)}, u32[]{:S(2)}) collective-permute-start(f32[320,256]{1,0:T(8,128)S(1)} %get-tuple-element.18), channel_id=1, source_target_pairs={{0,4},{1,5},{2,6},{3,7},{4,0},{5,1},{6,2},{7,3},{8,12},{9,13},{10,... | collective-permute-start | bytes 983048 | tf_op jit(solution)/shard_map/ppermute | solution.py:298
  421.6 25.8 %collective-permute-start.33 = (f32[320,256]{1,0:T(8,128)S(1)}, f32[320,256]{1,0:T(8,128)S(1)}, u32[]{:S(2)}, u32[]{:S(2)}) collective-permute-start(f32[320,256]{1,0:T(8,128)S(1)} %get-tuple-element.16), channel_id=1, source_target_pairs={{0,2},{1,3},{2,0},{3,1},{4,6},{5,7},{6,4},{7,5},{8,10},{9,11},{10,... | collective-permute-start | bytes 983048 | tf_op jit(solution)/shard_map/ppermute | solution.py:298
  448.6 14.8 %collective-permute-start.36 = (f32[320,256]{1,0:T(8,128)S(1)}, f32[320,256]{1,0:T(8,128)S(1)}, u32[]{:S(2)}, u32[]{:S(2)}) collective-permute-start(f32[320,256]{1,0:T(8,128)S(1)} %get-tuple-element.11), channel_id=1, source_target_pairs={{0,2},{1,3},{2,0},{3,1},{4,6},{5,7},{6,4},{7,5},{8,10},{9,11},{10,... | collective-permute-start | bytes 983048 | tf_op jit(solution)/shard_map/ppermute | solution.py:298
  450.8 14.8 %collective-permute-start.37 = (f32[320,256]{1,0:T(8,128)S(1)}, f32[320,256]{1,0:T(8,128)S(1)}, u32[]{:S(2)}, u32[]{:S(2)}) collective-permute-start(f32[320,256]{1,0:T(8,128)S(1)} %get-tuple-element.11), channel_id=1, source_target_pairs={{0,4},{1,5},{2,6},{3,7},{4,0},{5,1},{6,2},{7,3},{8,12},{9,13},{10,... | collective-permute-start | bytes 983048 | tf_op jit(solution)/shard_map/ppermute | solution.py:298
  451.8 28.1 %collective-permute-start.38 = (f32[320,256]{1,0:T(8,128)S(1)}, f32[320,256]{1,0:T(8,128)S(1)}, u32[]{:S(2)}, u32[]{:S(2)}) collective-permute-start(f32[320,256]{1,0:T(8,128)S(1)} %get-tuple-element.11), channel_id=1, source_target_pairs={{0,6},{1,7},{2,4},{3,5},{4,2},{5,3},{6,0},{7,1},{8,14},{9,15},{10,... | collective-permute-start | bytes 983048 | tf_op jit(solution)/shard_map/ppermute | solution.py:298
  479.9 4.7 collective-permute-start.39
  (14 other events, 27.5 us)

commit v2 on v1

--- a/solution.py
+++ b/solution.py
@@ -9,7 +9,12 @@
 
 AXES = ("band", "ga")
 F32, BF16 = jnp.float32, jnp.bfloat16
-PIECES = 2
+
+
+def bounds(d, n):
+    return (0, n // 2, 3 * n // 4, n) if d == 0 else (0, n // 2, n)
+
+
 CHUNKS = 2
 SUB = 256
 
@@ -35,7 +40,7 @@
 def invert_kernel(l_ref, *refs):
     outs, o_ref = refs[:-1], refs[-1]
     band, ga = lax.axis_index("band"), lax.axis_index("ga")
-    n, wide = l_ref.shape
+    _, wide = l_ref.shape
     o_ref[...] = l_ref[...]
 
     @pl.when(ga // 2 == band)
@@ -66,9 +71,10 @@
 
         loop(SUB.bit_length() - 2, lambda k: level(k + 1))
 
-    rows = n // len(outs)
-    for i, out in enumerate(outs):
-        out[...] = o_ref[pl.ds(i * rows, rows), :]
+    row = 0
+    for out in outs:
+        out[...] = o_ref[pl.ds(row, out.shape[0]), :]
+        row += out.shape[0]
 
 
 def pick_kernel(take_own, own_ref, *refs):
@@ -91,12 +97,13 @@
     return call(functools.partial(pick_kernel, take_own), own.shape, [own, *got], flops=own.size)
 
 
-def gather_kernel(take_own, pieces, *refs):
-    own, got, o_ref = refs[:pieces], refs[pieces:-1], refs[-1]
+def gather_kernel(take_own, pieces, got, *refs):
+    own, got, o_ref = refs[:pieces], refs[pieces : pieces + got], refs[-1]
     mine = take_own(lax.axis_index("band"), lax.axis_index("ga"))
-    rows = own[0].shape[0]
+    row = 0
     for i in range(pieces):
-        at = pl.ds(i * rows, rows)
+        at = pl.ds(row, own[i].shape[0])
+        row += own[i].shape[0]
 
         @pl.when(mine)
         def _():
@@ -110,11 +117,11 @@
             o_ref[at, :] = value
 
 
-def gathered(take_own, own, got):
+def gathered(take_own, own, got, after):
     shape = (sum(x.shape[0] for x in own), own[0].shape[1])
-    kernel = functools.partial(gather_kernel, take_own, len(own))
-    stages = len(got[0])
-    return call(kernel, shape, [*own, *(x[t] for t in range(stages) for x in got)], flops=2**20)
+    flat = [x[t] for t in range(len(got[0])) for x in got]
+    kernel = functools.partial(gather_kernel, take_own, len(own), len(flat))
+    return call(kernel, shape, [*own, *flat], after, flops=2**20)
 
 
 def fetch(blocks, lbuf, sem, core):
@@ -263,11 +270,12 @@
     return [[(s, b)] for b in range(s + 1, nb)]
 
 
-def tree(k, nq):
+def tree(b, k, nq):
     if nq == 4:
+        far = (b, k) in ((2, 0), (3, 0), (1, 0))
         return {
-            0: [[(0, 2)], [(0, 1), (2, 3)]],
-            1: [[(1, 2)], [(1, 0), (2, 3)]],
+            0: [[(0, 2)], [(0, 1), (2, 3)]] if far else [[(0, 3)], [(0, 1), (3, 2)]],
+            1: [[(1, 2)], [(1, 0), (2, 3)]] if b == 3 else [[(1, 3)], [(1, 0), (3, 2)]],
             2: [[(2, 3)], [(2, 0), (3, 1)]],
             3: [[(3, 1)], [(3, 2), (1, 0)]],
         }[k]
@@ -302,20 +310,22 @@
             x, [((b, q, c), (b, q, 1 - c)) for b in bands for q in range(nq) for c in range(2)]
         )
 
-    rows = n // PIECES
-    cut = lambda x: [x[i * rows : (i + 1) * rows] for i in range(PIECES)]
     ready = pl.pallas_call(
         invert_kernel,
-        out_shape=[jax.ShapeDtypeStruct((rows, lower.shape[1]), F32)] * PIECES,
+        out_shape=[
+            jax.ShapeDtypeStruct((z - a, lower.shape[1]), F32)
+            for a, z in zip(bounds(0, n), bounds(0, n)[1:])
+        ],
         in_specs=[VM],
-        out_specs=[VM] * PIECES,
+        out_specs=[VM] * (len(bounds(0, n)) - 1),
         scratch_shapes=[pltpu.VMEM(lower.shape, F32)],
         cost_estimate=pl.CostEstimate(flops=2**28, bytes_accessed=2**22, transcendentals=0),
     )(lower)
-    plain = lax.optimization_barrier(cut(lower))
+    limits = bounds(1, n)
+    plain = lax.optimization_barrier([lower[a:z] for a, z in zip(limits, limits[1:])])
 
     source = [ready] + [plain] * (nb - 1)
-    got = [[[] for _ in range(PIECES)] for _ in range(nb)]
+    got = [[[] for _ in source[d]] for d in range(nb)]
 
     def merged(d, i):
         if not got[d][i]:
@@ -324,20 +334,23 @@
 
     for t in range(stages(nq)):
         for d in range(nb):
-            for i in range(PIECES):
+            for i in range(len(source[d])):
                 hops = [
                     ((b, q, c), (b, to, c))
                     for b in range(d, nb)
-                    for q, to in tree(b - d, nq)[t]
+                    for q, to in tree(b, b - d, nq)[t]
                     for c in range(2)
-                    if d or c * (n // 2) < (i + 1) * rows
+                    if d or c * (n // 2) < bounds(0, n)[i + 1]
                 ]
                 got[d][i].append(shift(merged(d, i), hops))
     blocks = []
-    for d in range(nb):
-        mine = gathered(lambda band, ga: ga // 2 == band - d, source[d], got[d])
-        blocks.append(([mine], [swap(mine, range(d, nb))]))
-
+
+    def land(d, after):
+        own = lambda band, ga: ga // 2 == band - d
+        mine = gathered(own, source[d], got[d], after)
+        blocks.append(([mine], [swap(mine, range(nb))]))
+
+    land(0, [])
     wc = w // CHUNKS
     seen = [{} for _ in range(CHUNKS)]
     done = [[] for _ in range(CHUNKS)]
@@ -354,6 +367,8 @@
         )
 
     for s in range(nb):
+        if s:
+            land(s, [done[-1][s - 1]])
         for x in range(CHUNKS):
             rhs = psi[:, x * wc : (x + 1) * wc]
             if s > 1:

time: 490 us -> 565 us (1.15)
  waiting for transfers between devices: 243 us -> 367 us
  starting transfers between devices: 163 us -> 115 us
    ppermute x40 -> x42, waiting for transfers between devices: 243 us -> 367 us  [shift(): return lax.ppermute(x, AXES, pairs)]
    ppermute x40 -> x42, starting transfers between devices: 163 us -> 115 us  [shift(): return lax.ppermute(x, AXES, pairs)]
    unnamed x44 -> x66, local copies, waits for them, and re-layouts: 11 us -> 13.2 us
    pallas_call x26 -> x27, Pallas kernels: 58.9 us -> 58.2 us  [call(): pl.pallas_call(kernel, out_shape=jax.ShapeDtypeStruct(out_shape, F32), in...]
  transfers between devices with their start and end apart: 40 -> 42, of which waited for: 16 -> 21; matrix products, arithmetic and copies ran while one was open for 0% -> 0% of each run, Pallas kernels for 9% -> 7%
where the time goes in v2:
time: 565 us; the launch traced here: 564 us
  waiting for transfers between devices  367 us (65%)
  starting transfers between devices  115 us (20%)
  Pallas kernels  61.3 us (11%)
  local copies, waits for them, and re-layouts  15.3 us (3%)
    ppermute x42, waiting for transfers between devices, shift(): return lax.ppermute(x, AXES, pairs)  367 us
    ppermute x42, starting transfers between devices, shift(): return lax.ppermute(x, AXES, pairs)  115 us
    pallas_call x27, Pallas kernels, call(): pl.pallas_call(kernel, out_shape=jax.ShapeDtypeStruct(out_shape, F32), in...  58.2 us
    unnamed x66, local copies, waits for them, and re-layouts  13.2 us
  transfers between devices with their start and end apart: 42, of which 21 were waited for; matrix products, arithmetic and copies ran while one was open for 0% of the time, Pallas kernels for 7%

profile of v2, /device:TPU:15, one launch (start us, length us, event | category | flops | bytes accessed | tf_op | source)
XLA Modules:
  0.0 564.1 jit_solution(14752665225159190631)
XLA Ops:
  0.6 3.1 shard_map.41
  9.3 18.0 %collective-permute-done.1.refs_0_.refs_4_ = f32[256,512]{1,0:T(8,128)S(1)} collective-permute-done((f32[256,512]{1,0:T(8,128)}, f32[256,512]{1,0:T(8,128)S(1)}, u32[]{:S(2)}, u32[]{:S(2)}) %collective-permute-start.1) | collective-permute-done | bytes 524320 | tf_op jit(solution)/shard_map/ppermute | solution.py:306
  28.6 9.9 %collective-permute-done.2.refs_0_.refs_5_ = f32[256,512]{1,0:T(8,128)S(1)} collective-permute-done((f32[256,512]{1,0:T(8,128)}, f32[256,512]{1,0:T(8,128)S(1)}, u32[]{:S(2)}, u32[]{:S(2)}) %collective-permute-start.2) | collective-permute-done | bytes 524320 | tf_op jit(solution)/shard_map/ppermute | solution.py:306
  40.0 9.6 %collective-permute-done.5.refs_8_ = f32[256,512]{1,0:T(8,128)S(1)} collective-permute-done((f32[256,512]{1,0:T(8,128)S(1)}, f32[256,512]{1,0:T(8,128)S(1)}, u32[]{:S(2)}, u32[]{:S(2)}) %collective-permute-start.5) | collective-permute-done | bytes 524320 | tf_op jit(solution)/shard_map/ppermute | solution.py:306
  49.9 20.1 %collective-permute-start.6 = (f32[1024,512]{1,0:T(8,128)S(1)}, f32[1024,512]{1,0:T(8,128)S(1)}, u32[]{:S(2)}, u32[]{:S(2)}) collective-permute-start(f32[1024,512]{1,0:T(8,128)S(1)} %shard_map.45.refs_1_.refs_4_), channel_id=1, source_target_pairs={{0,1},{1,0},{2,3},{3,2},{4,5},{5,4},{6,7},{7,6},{8,9},{9,8},{10,11... | collective-permute-start | bytes 6291464 | tf_op jit(solution)/shard_map/ppermute | solution.py:306
  74.8 59.9 %collective-permute-done.12.refs_4_ = f32[512,512]{1,0:T(8,128)S(1)} collective-permute-done((f32[512,512]{1,0:T(8,128)S(1)}, f32[512,512]{1,0:T(8,128)S(1)}, u32[]{:S(2)}, u32[]{:S(2)}) %collective-permute-start.12) | collective-permute-done | bytes 1048608 | tf_op jit(solution)/shard_map/ppermute | solution.py:306
  134.7 22.9 %collective-permute-done.13.refs_5_ = f32[512,512]{1,0:T(8,128)S(1)} collective-permute-done((f32[512,512]{1,0:T(8,128)S(1)}, f32[512,512]{1,0:T(8,128)S(1)}, u32[]{:S(2)}, u32[]{:S(2)}) %collective-permute-start.13) | collective-permute-done | bytes 1048608 | tf_op jit(solution)/shard_map/ppermute | solution.py:306
  159.1 44.1 %collective-permute-start.21 = (f32[512,512]{1,0:T(8,128)S(1)}, f32[512,512]{1,0:T(8,128)S(1)}, u32[]{:S(2)}, u32[]{:S(2)}) collective-permute-start(f32[512,512]{1,0:T(8,128)S(1)} %get-tuple-element.10.own_ref.refs_0_), channel_id=1, source_target_pairs={{16,20},{17,21},{26,28},{27,29}} | collective-permute-start | bytes 3145736 | tf_op jit(solution)/shard_map/ppermute | solution.py:306
  205.3 20.3 %collective-permute-done.21.refs_0_.refs_2_ = f32[512,512]{1,0:T(8,128)S(1)} collective-permute-done((f32[512,512]{1,0:T(8,128)S(1)}, f32[512,512]{1,0:T(8,128)S(1)}, u32[]{:S(2)}, u32[]{:S(2)}) %collective-permute-start.21) | collective-permute-done | bytes 1048608 | tf_op jit(solution)/shard_map/ppermute | solution.py:306
  227.0 21.0 %collective-permute-done.22.refs_0_.refs_3_ = f32[512,512]{1,0:T(8,128)S(1)} collective-permute-done((f32[512,512]{1,0:T(8,128)S(1)}, f32[512,512]{1,0:T(8,128)S(1)}, u32[]{:S(2)}, u32[]{:S(2)}) %collective-permute-start.22) | collective-permute-done | bytes 1048608 | tf_op jit(solution)/shard_map/ppermute | solution.py:306
  251.2 20.1 %collective-permute-done.24.refs_5_ = f32[512,512]{1,0:T(8,128)S(1)} collective-permute-done((f32[512,512]{1,0:T(8,128)S(1)}, f32[512,512]{1,0:T(8,128)S(1)}, u32[]{:S(2)}, u32[]{:S(2)}) %collective-permute-start.24) | collective-permute-done | bytes 1048608 | tf_op jit(solution)/shard_map/ppermute | solution.py:306
  271.5 1.5 collective-permute-start.26
  274.5 1.7 collective-permute-start.20
  276.1 1.6 collective-permute-start.27
  282.6 1.6 collective-permute-start.9
  284.3 2.0 shard_map.58.refs_0_
  286.3 1.6 copy-done.21
  289.1 57.4 %collective-permute-done.18.refs_4_ = f32[512,512]{1,0:T(8,128)S(1)} collective-permute-done((f32[512,512]{1,0:T(8,128)S(1)}, f32[512,512]{1,0:T(8,128)S(1)}, u32[]{:S(2)}, u32[]{:S(2)}) %collective-permute-start.18) | collective-permute-done | bytes 1048608 | tf_op jit(solution)/shard_map/ppermute | solution.py:306
  346.5 22.5 %collective-permute-done.19.refs_5_ = f32[512,512]{1,0:T(8,128)S(1)} collective-permute-done((f32[512,512]{1,0:T(8,128)}, f32[512,512]{1,0:T(8,128)S(1)}, u32[]{:S(2)}, u32[]{:S(2)}) %collective-permute-start.19) | collective-permute-done | bytes 1048608 | tf_op jit(solution)/shard_map/ppermute | solution.py:306
  369.0 1.5 shard_map.60.refs_3_
  371.4 1.6 collective-permute-start.7
  373.0 2.2 shard_map.51
  375.3 1.7 collective-permute-start.29
  382.3 1.6 copy-done.18
  383.8 1.6 copy-done.26
  386.9 1.6 collective-permute-start.8
  389.7 14.2 %collective-permute-done.31.refs_1_ = f32[1024,256]{1,0:T(8,128)} collective-permute-done((f32[1024,256]{1,0:T(8,128)}, f32[1024,256]{1,0:T(8,128)}, u32[]{:S(2)}, u32[]{:S(2)}) %collective-permute-start.31) | collective-permute-done | bytes 1048608 | tf_op jit(solution)/shard_map/ppermute | solution.py:306
  406.5 9.9 %shard_map.65.refs_0_ = f32[1024,256]{1,0:T(8,128)S(1)} custom-call(f32[1024,256]{1,0:T(8,128)S(1)} %copy-done.8, f32[1024,256]{1,0:T(8,128)} %collective-permute-done.31.refs_1_, f32[1024,256]{1,0:T(8,128)} %collective-permute-done.32.refs_2_, f32[1024,512]{1,0:T(8,128)} %shard_map.60.refs_3_, f32[1024,512]{1,0:T(8,128)} %collective-permute-done.28.refs_4_, ...), custom_call_target="tpu_custom_call" | custom-call | flops 4831838208 | bytes 1048576 | tf_op jit(solution)/shard_map/pallas_call | solution.py:241
  416.4 9.9 %collective-permute-done.33.refs_1_ = f32[1024,256]{1,0:T(8,128)S(1)} collective-permute-done((f32[1024,256]{1,0:T(8,128)}, f32[1024,256]{1,0:T(8,128)S(1)}, u32[]{:S(2)}, u32[]{:S(2)}) %collective-permute-start.33) | collective-permute-done | bytes 1048608 | tf_op jit(solution)/shard_map/ppermute | solution.py:306
  427.3 1.6 copy-done.23
  430.1 7.6 %shard_map.66 = f32[1024,256]{1,0:T(8,128)S(1)} custom-call(f32[1024,256]{1,0:T(8,128)S(1)} %shard_map.65.refs_0_, f32[1024,256]{1,0:T(8,128)S(1)} %copy-done.29, f32[1024,512]{1,0:T(8,128)S(1)} %copy-done.16, f32[1024,512]{1,0:T(8,128)S(1)} %copy-done.23, f32[1024,512]{1,0:T(8,128)S(1)} %shard_map.45.refs_1_.refs_4_, f32[1024,512]{1,0:T(8,128)S(1)} %copy-done.1), custom_call_target="tpu_custom_call" | custom-call | flops 3221225472 | bytes 1048576 | tf_op jit(solution)/shard_map/pallas_call | solution.py:241
  439.1 9.8 %collective-permute-done.8.refs_1_ = f32[1024,256]{1,0:T(8,128)} collective-permute-done((f32[1024,256]{1,0:T(8,128)}, f32[1024,256]{1,0:T(8,128)}, u32[]{:S(2)}, u32[]{:S(2)}) %collective-permute-start.8) | collective-permute-done | bytes 1048608 | tf_op jit(solution)/shard_map/ppermute | solution.py:306
  448.8 9.9 %shard_map.61.refs_0_ = f32[1024,256]{1,0:T(8,128)S(1)} custom-call(f32[1024,256]{1,0:T(8,128)S(1)} %copy-done.6, f32[1024,256]{1,0:T(8,128)} %collective-permute-done.8.refs_1_, f32[1024,256]{1,0:T(8,128)} %collective-permute-done.15.refs_2_, f32[1024,512]{1,0:T(8,128)} %shard_map.60.refs_3_, f32[1024,512]{1,0:T(8,128)} %collective-permute-done.28.refs_4_, ...), custom_call_target="tpu_custom_call" | custom-call | flops 4831838208 | bytes 1048576 | tf_op jit(solution)/shard_map/pallas_call | solution.py:241
  458.7 12.6 %collective-permute-done.30.refs_1_ = f32[1024,256]{1,0:T(8,128)} collective-permute-done((f32[1024,256]{1,0:T(8,128)S(1)}, f32[1024,256]{1,0:T(8,128)}, u32[]{:S(2)}, u32[]{:S(2)}) %collective-permute-start.30) | collective-permute-done | bytes 1048608 | tf_op jit(solution)/shard_map/ppermute | solution.py:306
  471.3 8.9 %shard_map.64 = f32[1024,256]{1,0:T(8,128)S(1)} custom-call(f32[1024,256]{1,0:T(8,128)S(1)} %shard_map.61.refs_0_, f32[1024,256]{1,0:T(8,128)} %collective-permute-done.30.refs_1_, f32[1024,512]{1,0:T(8,128)S(1)} %copy-done.16, f32[1024,512]{1,0:T(8,128)S(1)} %copy-done.24, f32[1024,512]{1,0:T(8,128)S(1)} %shard_map.45.refs_1_.refs_4_, f32[1024,512]{1,0:T(8,128)S(1)} %copy-done.1), custom_call_target="tpu_custom_call" | custom-call | flops 3221225472 | bytes 1048576 | tf_op jit(solution)/shard_map/pallas_call | solution.py:241
  480.2 1.6 select_select_fusion.1
  482.1 4.5 shard_map.67
  486.6 1.5 copy-done.11
  490.1 2.9 collective-permute-done.34
  493.0 1.5 dynamic-slice_add_fusion
  497.2 21.0 %collective-permute-done.37 = f32[320,256]{1,0:T(8,128)S(1)} collective-permute-done((f32[320,256]{1,0:T(8,128)S(1)}, f32[320,256]{1,0:T(8,128)S(1)}, u32[]{:S(2)}, u32[]{:S(2)}) %collective-permute-start.37) | collective-permute-done | bytes 327712 | tf_op jit(solution)/shard_map/ppermute | solution.py:306
  518.2 4.0 collective-permute-done.36
  522.3 4.3 collective-permute-start.38
  527.9 10.4 %collective-permute-done.38 = f32[320,256]{1,0:T(8,128)S(1)} collective-permute-done((f32[320,256]{1,0:T(8,128)S(1)}, f32[320,256]{1,0:T(8,128)S(1)}, u32[]{:S(2)}, u32[]{:S(2)}) %collective-permute-start.38) | collective-permute-done | bytes 327712 | tf_op jit(solution)/shard_map/ppermute | solution.py:306
  538.4 2.0 collective-permute-done.39
  540.3 16.0 %collective-permute-done.40 = f32[320,256]{1,0:T(8,128)S(1)} collective-permute-done((f32[320,256]{1,0:T(8,128)S(1)}, f32[320,256]{1,0:T(8,128)S(1)}, u32[]{:S(2)}, u32[]{:S(2)}) %collective-permute-start.40) | collective-permute-done | bytes 327712 | tf_op jit(solution)/shard_map/ppermute | solution.py:306
  558.1 2.4 collective-permute-done.41
  560.5 3.5 shard_map.68
  (146 shorter events, 52.1 us)
Async XLA Ops:
  3.7 3.3 collective-permute-start
  4.5 22.8 %collective-permute-start.1 = (f32[256,512]{1,0:T(8,128)}, f32[256,512]{1,0:T(8,128)S(1)}, u32[]{:S(2)}, u32[]{:S(2)}) collective-permute-start(f32[256,512]{1,0:T(8,128)} %get-tuple-element.8.own_ref.refs_1_), channel_id=1, source_target_pairs={{0,6},{1,7},{10,14},{11,15},{20,22},{21,23},{30,26},{31,27}} | collective-permute-start | bytes 1572872 | tf_op jit(solution)/shard_map/ppermute | solution.py:306
  5.8 32.8 %collective-permute-start.2 = (f32[256,512]{1,0:T(8,128)}, f32[256,512]{1,0:T(8,128)S(1)}, u32[]{:S(2)}, u32[]{:S(2)}) collective-permute-start(f32[256,512]{1,0:T(8,128)} %get-tuple-element.9.own_ref.refs_2_), channel_id=1, source_target_pairs={{0,6},{1,7},{10,14},{11,15},{20,22},{21,23},{30,26},{31,27}} | collective-permute-start | bytes 1572872 | tf_op jit(solution)/shard_map/ppermute | solution.py:306
  8.4 41.3 %copy-start.10 = (f32[512,512]{1,0:T(8,128)S(1)}, f32[512,512]{1,0:T(8,128)}, u32[]{:S(2)}) copy-start(f32[512,512]{1,0:T(8,128)} %get-tuple-element.7.own_ref.refs_0_) | copy-start | bytes 3145732
  8.4 41.3 %collective-permute-start.3 = (f32[512,512]{1,0:T(8,128)S(1)}, f32[512,512]{1,0:T(8,128)S(1)}, u32[]{:S(2)}, u32[]{:S(2)}) collective-permute-start(f32[512,512]{1,0:T(8,128)S(1)} %shard_map.42), channel_id=1, source_target_pairs={{0,2},{6,4},{10,8},{14,12},{20,16},{22,18},{30,28},{26,24}} | collective-permute-start | bytes 3145736 | tf_op jit(solution)/shard_map/ppermute | solution.py:306
  27.3 12.7 %collective-permute-start.4 = (f32[256,512]{1,0:T(8,128)S(1)}, f32[256,512]{1,0:T(8,128)S(1)}, u32[]{:S(2)}, u32[]{:S(2)}) collective-permute-start(f32[256,512]{1,0:T(8,128)S(1)} %shard_map.43), channel_id=1, source_target_pairs={{0,2},{1,3},{6,4},{7,5},{10,8},{11,9},{14,12},{15,13},{20,16},{21,... | collective-permute-start | bytes 1572872 | tf_op jit(solution)/shard_map/ppermute | solution.py:306
  38.6 11.1 %collective-permute-start.5 = (f32[256,512]{1,0:T(8,128)S(1)}, f32[256,512]{1,0:T(8,128)S(1)}, u32[]{:S(2)}, u32[]{:S(2)}) collective-permute-start(f32[256,512]{1,0:T(8,128)S(1)} %shard_map.44), channel_id=1, source_target_pairs={{0,2},{1,3},{6,4},{7,5},{10,8},{11,9},{14,12},{15,13},{20,16},{21,... | collective-permute-start | bytes 1572872 | tf_op jit(solution)/shard_map/ppermute | solution.py:306
  49.9 24.9 %collective-permute-start.6 = (f32[1024,512]{1,0:T(8,128)S(1)}, f32[1024,512]{1,0:T(8,128)S(1)}, u32[]{:S(2)}, u32[]{:S(2)}) collective-permute-start(f32[1024,512]{1,0:T(8,128)S(1)} %shard_map.45.refs_1_.refs_4_), channel_id=1, source_target_pairs={{0,1},{1,0},{2,3},{3,2},{4,5},{5,4},{6,7},{7,6},{8,9},{9,8},{10,11... | collective-permute-start | bytes 6291464 | tf_op jit(solution)/shard_map/ppermute | solution.py:306
  70.1 1.5 collective-permute-start.10
  70.9 2.3 collective-permute-start.11
  71.7 63.0 %collective-permute-start.12 = (f32[512,512]{1,0:T(8,128)S(1)}, f32[512,512]{1,0:T(8,128)S(1)}, u32[]{:S(2)}, u32[]{:S(2)}) collective-permute-start(f32[512,512]{1,0:T(8,128)S(1)} %shard_map.47), channel_id=1, source_target_pairs={{8,10},{9,11},{12,14},{13,15},{18,16},{19,17},{22,20},{23,21},{28,... | collective-permute-start | bytes 3145736 | tf_op jit(solution)/shard_map/ppermute | solution.py:306
  73.3 84.4 %collective-permute-start.13 = (f32[512,512]{1,0:T(8,128)S(1)}, f32[512,512]{1,0:T(8,128)S(1)}, u32[]{:S(2)}, u32[]{:S(2)}) collective-permute-start(f32[512,512]{1,0:T(8,128)S(1)} %shard_map.48), channel_id=1, source_target_pairs={{8,10},{9,11},{12,14},{13,15},{18,16},{19,17},{22,20},{23,21},{28,... | collective-permute-start | bytes 3145736 | tf_op jit(solution)/shard_map/ppermute | solution.py:306
  74.8 209.5 %copy-start.7 = (f32[1024,256]{1,0:T(8,128)}, f32[1024,256]{1,0:T(8,128)S(1)}, u32[]{:S(2)}) copy-start(f32[1024,256]{1,0:T(8,128)S(1)} %get-tuple-element.15.refs_0_) | copy-start | bytes 3145732
  74.8 298.3 %copy-start.4 = (f32[1024,256]{1,0:T(8,128)}, f32[1024,256]{1,0:T(8,128)S(1)}, u32[]{:S(2)}) copy-start(f32[1024,256]{1,0:T(8,128)S(1)} %get-tuple-element.14.refs_0_) | copy-start | bytes 3145732
  74.8 298.3 %copy-start = (f32[1024,512]{1,0:T(8,128)}, f32[1024,512]{1,0:T(8,128)S(1)}, u32[]{:S(2)}) copy-start(f32[1024,512]{1,0:T(8,128)S(1)} %collective-permute-done.6.refs_2_.refs_5_) | copy-start | bytes 6291460
  157.9 215.2 %copy-start.15 = (f32[1024,512]{1,0:T(8,128)}, f32[1024,512]{1,0:T(8,128)S(1)}, u32[]{:S(2)}) copy-start(f32[1024,512]{1,0:T(8,128)S(1)} %shard_map.50.refs_2_) | copy-start | bytes 6291460
  157.9 91.6 %collective-permute-start.14 = (f32[1024,512]{1,0:T(8,128)S(1)}, f32[1024,512]{1,0:T(8,128)S(1)}, u32[]{:S(2)}, u32[]{:S(2)}) collective-permute-start(f32[1024,512]{1,0:T(8,128)S(1)} %shard_map.50.refs_2_), channel_id=1, source_target_pairs={{0,1},{1,0},{2,3},{3,2},{4,5},{5,4},{6,7},{7,6},{8,9},{9,8},{10,11... | collective-permute-start | bytes 6291464 | tf_op jit(solution)/shard_map/ppermute | solution.py:306
  159.1 66.5 %collective-permute-start.21 = (f32[512,512]{1,0:T(8,128)S(1)}, f32[512,512]{1,0:T(8,128)S(1)}, u32[]{:S(2)}, u32[]{:S(2)}) collective-permute-start(f32[512,512]{1,0:T(8,128)S(1)} %get-tuple-element.10.own_ref.refs_0_), channel_id=1, source_target_pairs={{16,20},{17,21},{26,28},{27,29}} | collective-permute-start | bytes 3145736 | tf_op jit(solution)/shard_map/ppermute | solution.py:306
  203.2 44.9 %collective-permute-start.22 = (f32[512,512]{1,0:T(8,128)S(1)}, f32[512,512]{1,0:T(8,128)S(1)}, u32[]{:S(2)}, u32[]{:S(2)}) collective-permute-start(f32[512,512]{1,0:T(8,128)S(1)} %get-tuple-element.11.own_ref.refs_1_), channel_id=1, source_target_pairs={{16,20},{17,21},{26,28},{27,29}} | collective-permute-start | bytes 3145736 | tf_op jit(solution)/shard_map/ppermute | solution.py:306
  204.5 45.0 %collective-permute-start.25 = (f32[1024,256]{1,0:T(8,128)S(1)}, f32[1024,256]{1,0:T(8,128)S(1)}, u32[]{:S(2)}, u32[]{:S(2)}) collective-permute-start(f32[1024,256]{1,0:T(8,128)S(1)} %shard_map.49.refs_6_), channel_id=1, source_target_pairs={{0,8},{1,9},{2,10},{3,11},{4,12},{5,13},{6,14},{7,15}} | collective-permute-start | bytes 3145736 | tf_op jit(solution)/shard_map/ppermute | solution.py:306
  225.7 25.5 %collective-permute-start.23 = (f32[512,512]{1,0:T(8,128)S(1)}, f32[512,512]{1,0:T(8,128)S(1)}, u32[]{:S(2)}, u32[]{:S(2)}) collective-permute-start(f32[512,512]{1,0:T(8,128)S(1)} %shard_map.54), channel_id=1, source_target_pairs={{16,18},{17,19},{20,22},{21,23},{26,24},{27,25},{28,30},{29,31}} | collective-permute-start | bytes 3145736 | tf_op jit(solution)/shard_map/ppermute | solution.py:306
  248.1 23.2 %collective-permute-start.24 = (f32[512,512]{1,0:T(8,128)S(1)}, f32[512,512]{1,0:T(8,128)S(1)}, u32[]{:S(2)}, u32[]{:S(2)}) collective-permute-start(f32[512,512]{1,0:T(8,128)S(1)} %shard_map.55), channel_id=1, source_target_pairs={{16,18},{17,19},{20,22},{21,23},{26,24},{27,25},{28,30},{29,31}} | collective-permute-start | bytes 3145736 | tf_op jit(solution)/shard_map/ppermute | solution.py:306
  271.5 12.8 %collective-permute-start.26 = (f32[1024,512]{1,0:T(8,128)S(1)}, f32[1024,512]{1,0:T(8,128)S(1)}, u32[]{:S(2)}, u32[]{:S(2)}) collective-permute-start(f32[1024,512]{1,0:T(8,128)S(1)} %shard_map.57.refs_2_.refs_5_), channel_id=1, source_target_pairs={{0,1},{1,0},{2,3},{3,2},{4,5},{5,4},{6,7},{7,6},{8,9},{9,8},{10,11... | collective-permute-start | bytes 6291464 | tf_op jit(solution)/shard_map/ppermute | solution.py:306
  273.0 4.8 collective-permute-start.16
  273.7 5.4 collective-permute-start.17
  274.5 8.1 %collective-permute-start.20 = (f32[1024,256]{1,0:T(8,128)S(1)}, f32[1024,256]{1,0:T(8,128)}, u32[]{:S(2)}, u32[]{:S(2)}) collective-permute-start(f32[1024,256]{1,0:T(8,128)S(1)} %shard_map.49.refs_6_), channel_id=1, source_target_pairs={{0,16},{1,17},{2,18},{3,19},{4,20},{5,21},{6,22},{7,23}} | collective-permute-start | bytes 3145736 | tf_op jit(solution)/shard_map/ppermute | solution.py:306
  276.1 10.1 %collective-permute-start.27 = (f32[1024,256]{1,0:T(8,128)}, f32[1024,256]{1,0:T(8,128)}, u32[]{:S(2)}, u32[]{:S(2)}) collective-permute-start(f32[1024,256]{1,0:T(8,128)} %shard_map.56.refs_6_), channel_id=1, source_target_pairs={{8,16},{9,17},{10,18},{11,19},{12,20},{13,21},{14,22},{15,23}} | collective-permute-start | bytes 3145736 | tf_op jit(solution)/shard_map/ppermute | solution.py:306
  277.9 68.6 %collective-permute-start.18 = (f32[512,512]{1,0:T(8,128)S(1)}, f32[512,512]{1,0:T(8,128)S(1)}, u32[]{:S(2)}, u32[]{:S(2)}) collective-permute-start(f32[512,512]{1,0:T(8,128)S(1)} %shard_map.52), channel_id=1, source_target_pairs={{24,26},{25,27},{28,30},{29,31}} | collective-permute-start | bytes 3145736 | tf_op jit(solution)/shard_map/ppermute | solution.py:306
  280.2 88.7 %collective-permute-start.19 = (f32[512,512]{1,0:T(8,128)}, f32[512,512]{1,0:T(8,128)S(1)}, u32[]{:S(2)}, u32[]{:S(2)}) collective-permute-start(f32[512,512]{1,0:T(8,128)} %shard_map.53), channel_id=1, source_target_pairs={{24,26},{25,27},{28,30},{29,31}} | collective-permute-start | bytes 3145736 | tf_op jit(solution)/shard_map/ppermute | solution.py:306
  282.6 90.4 %collective-permute-start.9 = (f32[1024,256]{1,0:T(8,128)}, f32[1024,256]{1,0:T(8,128)}, u32[]{:S(2)}, u32[]{:S(2)}) collective-permute-start(f32[1024,256]{1,0:T(8,128)} %shard_map.46), channel_id=1, source_target_pairs={{0,8},{1,9},{2,10},{3,11},{4,12},{5,13},{6,14},{7,15}} | collective-permute-start | bytes 3145736 | tf_op jit(solution)/shard_map/ppermute | solution.py:306
  289.1 81.4 %copy-start.2 = (f32[1024,256]{1,0:T(8,128)}, f32[1024,256]{1,0:T(8,128)S(1)}, u32[]{:S(2)}) copy-start(f32[1024,256]{1,0:T(8,128)S(1)} %shard_map.59.refs_6_) | copy-start | bytes 3145732
  370.5 36.0 %collective-permute-start.28 = (f32[1024,512]{1,0:T(8,128)}, f32[1024,512]{1,0:T(8,128)}, u32[]{:S(2)}, u32[]{:S(2)}) collective-permute-start(f32[1024,512]{1,0:T(8,128)} %shard_map.60.refs_3_), channel_id=1, source_target_pairs={{0,1},{1,0},{2,3},{3,2},{4,5},{5,4},{6,7},{7,6},{8,9},{9,8},{10,11... | collective-permute-start | bytes 6291464 | tf_op jit(solution)/shard_map/ppermute | solution.py:306
  371.4 8.2 %collective-permute-start.7 = (f32[1024,256]{1,0:T(8,128)}, f32[1024,256]{1,0:T(8,128)}, u32[]{:S(2)}, u32[]{:S(2)}) collective-permute-start(f32[1024,256]{1,0:T(8,128)} %shard_map.46), channel_id=1, source_target_pairs={{0,16},{1,17},{2,18},{3,19},{4,20},{5,21},{6,22},{7,23}} | collective-permute-start | bytes 3145736 | tf_op jit(solution)/shard_map/ppermute | solution.py:306
  375.3 11.6 %collective-permute-start.29 = (f32[1024,256]{1,0:T(8,128)}, f32[1024,256]{1,0:T(8,128)}, u32[]{:S(2)}, u32[]{:S(2)}) collective-permute-start(f32[1024,256]{1,0:T(8,128)} %shard_map.51), channel_id=1, source_target_pairs={{8,16},{9,17},{10,18},{11,19},{12,20},{13,21},{14,22},{15,23}} | collective-permute-start | bytes 3145736 | tf_op jit(solution)/shard_map/ppermute | solution.py:306
  377.0 26.9 %collective-permute-start.31 = (f32[1024,256]{1,0:T(8,128)}, f32[1024,256]{1,0:T(8,128)}, u32[]{:S(2)}, u32[]{:S(2)}) collective-permute-start(f32[1024,256]{1,0:T(8,128)} %collective-permute-done.20.refs_1_), channel_id=1, source_target_pairs={{16,24},{17,25},{18,26},{19,27},{20,28},{21,29},{22,30},{23,31}} | collective-permute-start | bytes 3145736 | tf_op jit(solution)/shard_map/ppermute | solution.py:306
  378.2 26.9 %collective-permute-start.32 = (f32[1024,256]{1,0:T(8,128)}, f32[1024,256]{1,0:T(8,128)}, u32[]{:S(2)}, u32[]{:S(2)}) collective-permute-start(f32[1024,256]{1,0:T(8,128)} %shard_map.56.refs_6_), channel_id=1, source_target_pairs={{8,24},{9,25},{10,26},{11,27},{12,28},{13,29},{14,30},{15,31}} | collective-permute-start | bytes 3145736 | tf_op jit(solution)/shard_map/ppermute | solution.py:306
  379.6 46.7 %collective-permute-start.33 = (f32[1024,256]{1,0:T(8,128)}, f32[1024,256]{1,0:T(8,128)S(1)}, u32[]{:S(2)}, u32[]{:S(2)}) collective-permute-start(f32[1024,256]{1,0:T(8,128)} %copy-done.2), channel_id=1, source_target_pairs={{16,24},{17,25},{18,26},{19,27},{20,28},{21,29},{22,30},{23,31}} | collective-permute-start | bytes 3145736 | tf_op jit(solution)/shard_map/ppermute | solution.py:306
  386.9 62.0 %collective-permute-start.8 = (f32[1024,256]{1,0:T(8,128)}, f32[1024,256]{1,0:T(8,128)}, u32[]{:S(2)}, u32[]{:S(2)}) collective-permute-start(f32[1024,256]{1,0:T(8,128)} %collective-permute-done.7.refs_1_), channel_id=1, source_target_pairs={{16,24},{17,25},{18,26},{19,27},{20,28},{21,29},{22,30},{23,31}} | collective-permute-start | bytes 3145736 | tf_op jit(solution)/shard_map/ppermute | solution.py:306
  403.9 44.9 %collective-permute-start.15 = (f32[1024,256]{1,0:T(8,128)}, f32[1024,256]{1,0:T(8,128)}, u32[]{:S(2)}, u32[]{:S(2)}) collective-permute-start(f32[1024,256]{1,0:T(8,128)} %shard_map.51), channel_id=1, source_target_pairs={{8,24},{9,25},{10,26},{11,27},{12,28},{13,29},{14,30},{15,31}} | collective-permute-start | bytes 3145736 | tf_op jit(solution)/shard_map/ppermute | solution.py:306
  405.2 66.1 %collective-permute-start.30 = (f32[1024,256]{1,0:T(8,128)S(1)}, f32[1024,256]{1,0:T(8,128)}, u32[]{:S(2)}, u32[]{:S(2)}) collective-permute-start(f32[1024,256]{1,0:T(8,128)S(1)} %shard_map.63), channel_id=1, source_target_pairs={{16,24},{17,25},{18,26},{19,27},{20,28},{21,29},{22,30},{23,31}} | collective-permute-start | bytes 3145736 | tf_op jit(solution)/shard_map/ppermute | solution.py:306
  489.2 3.7 collective-permute-start.34
  494.5 23.7 %collective-permute-start.37 = (f32[320,256]{1,0:T(8,128)S(1)}, f32[320,256]{1,0:T(8,128)S(1)}, u32[]{:S(2)}, u32[]{:S(2)}) collective-permute-start(f32[320,256]{1,0:T(8,128)S(1)} %get-tuple-element.19), channel_id=1, source_target_pairs={{0,6},{1,7},{2,4},{3,5},{4,2},{5,3},{6,0},{7,1},{8,14},{9,15},{10,... | collective-permute-start | bytes 983048 | tf_op jit(solution)/shard_map/ppermute | solution.py:306
  494.6 27.5 %collective-permute-start.36 = (f32[320,256]{1,0:T(8,128)S(1)}, f32[320,256]{1,0:T(8,128)S(1)}, u32[]{:S(2)}, u32[]{:S(2)}) collective-permute-start(f32[320,256]{1,0:T(8,128)S(1)} %get-tuple-element.20), channel_id=1, source_target_pairs={{0,4},{1,5},{2,6},{3,7},{4,0},{5,1},{6,2},{7,3},{8,12},{9,13},{10,... | collective-permute-start | bytes 983048 | tf_op jit(solution)/shard_map/ppermute | solution.py:306
  496.0 26.2 %collective-permute-start.35 = (f32[320,256]{1,0:T(8,128)S(1)}, f32[320,256]{1,0:T(8,128)S(1)}, u32[]{:S(2)}, u32[]{:S(2)}) collective-permute-start(f32[320,256]{1,0:T(8,128)S(1)} %get-tuple-element.18), channel_id=1, source_target_pairs={{0,2},{1,3},{2,0},{3,1},{4,6},{5,7},{6,4},{7,5},{8,10},{9,11},{10,... | collective-permute-start | bytes 983048 | tf_op jit(solution)/shard_map/ppermute | solution.py:306
  522.3 16.0 %collective-permute-start.38 = (f32[320,256]{1,0:T(8,128)S(1)}, f32[320,256]{1,0:T(8,128)S(1)}, u32[]{:S(2)}, u32[]{:S(2)}) collective-permute-start(f32[320,256]{1,0:T(8,128)S(1)} %get-tuple-element.13), channel_id=1, source_target_pairs={{0,2},{1,3},{2,0},{3,1},{4,6},{5,7},{6,4},{7,5},{8,10},{9,11},{10,... | collective-permute-start | bytes 983048 | tf_op jit(solution)/shard_map/ppermute | solution.py:306
  526.7 13.7 %collective-permute-start.39 = (f32[320,256]{1,0:T(8,128)S(1)}, f32[320,256]{1,0:T(8,128)S(1)}, u32[]{:S(2)}, u32[]{:S(2)}) collective-permute-start(f32[320,256]{1,0:T(8,128)S(1)} %get-tuple-element.13), channel_id=1, source_target_pairs={{0,4},{1,5},{2,6},{3,7},{4,0},{5,1},{6,2},{7,3},{8,12},{9,13},{10,... | collective-permute-start | bytes 983048 | tf_op jit(solution)/shard_map/ppermute | solution.py:306
  526.7 29.7 %collective-permute-start.40 = (f32[320,256]{1,0:T(8,128)S(1)}, f32[320,256]{1,0:T(8,128)S(1)}, u32[]{:S(2)}, u32[]{:S(2)}) collective-permute-start(f32[320,256]{1,0:T(8,128)S(1)} %get-tuple-element.13), channel_id=1, source_target_pairs={{0,6},{1,7},{2,4},{3,5},{4,2},{5,3},{6,0},{7,1},{8,14},{9,15},{10,... | collective-permute-start | bytes 983048 | tf_op jit(solution)/shard_map/ppermute | solution.py:306
  556.4 4.1 collective-permute-start.41
  (27 other events, 248.3 us)

commit v3 on v0

--- a/solution.py
+++ b/solution.py
@@ -9,7 +9,12 @@
 
 AXES = ("band", "ga")
 F32, BF16 = jnp.float32, jnp.bfloat16
-PIECES = 2
+
+
+def bounds(d, n):
+    return (0, n // 2, 3 * n // 4, n) if d == "first" else (0, n // 2, n)
+
+
 CHUNKS = 2
 SUB = 256
 
@@ -35,7 +40,7 @@
 def invert_kernel(l_ref, *refs):
     outs, o_ref = refs[:-1], refs[-1]
     band, ga = lax.axis_index("band"), lax.axis_index("ga")
-    n, wide = l_ref.shape
+    _, wide = l_ref.shape
     o_ref[...] = l_ref[...]
 
     @pl.when(ga // 2 == band)
@@ -66,29 +71,48 @@
 
         loop(SUB.bit_length() - 2, lambda k: level(k + 1))
 
-    rows = n // len(outs)
-    for i, out in enumerate(outs):
-        out[...] = o_ref[pl.ds(i * rows, rows), :]
-
-
-def pick_kernel(take_own, own_ref, *refs):
-    got, o_ref = refs[:-1], refs[-1]
-    mine = take_own(lax.axis_index("band"), lax.axis_index("ga"))
-
-    @pl.when(mine)
-    def _():
-        o_ref[...] = own_ref[...]
-
-    @pl.when(jnp.logical_not(mine))
-    def _():
-        value = got[0][...]
-        for ref in got[1:]:
-            value = value + ref[...]
-        o_ref[...] = value
-
-
-def pick(take_own, own, *got):
-    return call(functools.partial(pick_kernel, take_own), own.shape, [own, *got], flops=own.size)
+    row = 0
+    for out in outs:
+        out[...] = o_ref[pl.ds(row, out.shape[0]), :]
+        row += out.shape[0]
+
+
+def choose_kernel(rules, pieces, *refs):
+    o_ref = refs[-1]
+    chip, band = lax.axis_index("ga") // 2, lax.axis_index("band")
+    for u, rule in enumerate(rules):
+
+        @pl.when(rule(band, chip))
+        def _():
+            row = 0
+            for ref in refs[u * pieces : (u + 1) * pieces]:
+                o_ref[pl.ds(row, ref.shape[0]), :] = ref[...]
+                row += ref.shape[0]
+
+
+def choose(rules, sources, after=()):
+    pieces = len(sources[0])
+    shape = (sum(x.shape[0] for x in sources[0]), sources[0][0].shape[1])
+    given = [x for source in sources for x in source]
+
+    def kernel(*refs):
+        choose_kernel(rules, pieces, *refs[: len(given)], refs[-1])
+
+    return call(kernel, shape, given, after, flops=2**20)
+
+
+def taken(ks, stage, bit, nq):
+    def rule(band, chip):
+        found = False
+        for k in ks:
+            x = chip ^ (band - k)
+            hit = x == 0 if stage < 0 else (x & -x) == (nq >> (stage + 1))
+            if bit:
+                hit = hit & ((x & (2 * bit - 1)) == 0)
+            found = hit if found is False else found | hit
+        return found
+
+    return rule
 
 
 def fetch(blocks, lbuf, sem, core):
@@ -125,11 +149,11 @@
     loop(n // SUB * (n // depth), body)
 
 
-def band_kernel(s, final, pieces, given, *refs):
+def band_kernel(s, final, pieces, given, after, *refs):
     r_ref, y_refs, refs = refs[0], refs[1 : 1 + given], refs[1 + given :]
     nblocks = given + (1 if final else 0)
     blocks = unflatten(refs[: nblocks * 2 * pieces], pieces)
-    o_ref, lbuf, yh, yl, sem = refs[nblocks * 2 * pieces :]
+    o_ref, lbuf, yh, yl, sem = refs[nblocks * 2 * pieces + after :]
     band, core = lax.axis_index("band"), lax.axis_index("ga") % 2
     n = lbuf.shape[1]
 
@@ -231,13 +255,9 @@
     return [piece for mine, other in blocks for piece in mine + other]
 
 
-def pick_band(a, own, other):
-    return pick(lambda band, ga: band == a, own, other)
-
-
 def routes(s, nb):
     if nb == 4:
-        return {0: [[(0, 1)], [(0, 2), (1, 3)]], 1: [[(1, 2)], [(1, 3)]], 2: [[(2, 3)]]}[s]
+        return {0: [[(0, 1)], [(0, 2)], [(2, 3)]], 1: [[(1, 2)], [(1, 3)]], 2: [[(2, 3)]]}[s]
     return [[(s, b)] for b in range(s + 1, nb)]
 
 
@@ -264,71 +284,83 @@
             x, [((b, q, c), (b, q, 1 - c)) for b in bands for q in range(nq) for c in range(2)]
         )
 
-    rows = n // PIECES
-    cut = lambda x: [x[i * rows : (i + 1) * rows] for i in range(PIECES)]
     ready = pl.pallas_call(
         invert_kernel,
-        out_shape=[jax.ShapeDtypeStruct((rows, lower.shape[1]), F32)] * PIECES,
+        out_shape=[
+            jax.ShapeDtypeStruct((z - a, lower.shape[1]), F32)
+            for a, z in zip(bounds("first", n), bounds("first", n)[1:])
+        ],
         in_specs=[VM],
-        out_specs=[VM] * PIECES,
+        out_specs=[VM] * (len(bounds("first", n)) - 1),
         scratch_shapes=[pltpu.VMEM(lower.shape, F32)],
         cost_estimate=pl.CostEstimate(flops=2**28, bytes_accessed=2**22, transcendentals=0),
     )(lower)
-    plain = lax.optimization_barrier(cut(lower))
-
-    source = [ready] + [plain] * (nb - 1)
-    got = [[[] for _ in range(PIECES)] for _ in range(nb)]
-
-    def merged(d, i):
-        if not got[d][i]:
-            return source[d][i]
-        return pick(lambda band, ga: ga // 2 == band - d, source[d][i], *got[d][i])
+
+    sets = {"first": (range(1), (0,)), "near": (range(1, nb), (0, 1))}
+    sets.update({d: (range(d, nb), (d,)) for d in range(2, nb)})
+    limits = bounds("near", n)
+    plain = lax.optimization_barrier([lower[a:z] for a, z in zip(limits, limits[1:])])
+    source = {d: plain for d in sets}
+    source["first"] = ready
+    source["near"] = [ready[0], choose([lambda band, chip: band >= 0], [ready[1:]])]
+    got = {d: [[] for _ in source[d]] for d in sets}
 
     for t in range(stages(nq)):
         bit = nq >> (t + 1)
-        for d in range(nb):
-            for i in range(PIECES):
-                hops = []
-                for b in range(d, nb):
-                    for q in range(nq):
-                        if (q ^ (b - d)) & (2 * bit - 1) == 0:
-                            for c in range(2):
-                                if d or c * (n // 2) < (i + 1) * rows:
-                                    hops.append(((b, q, c), (b, q ^ bit, c)))
-                got[d][i].append(shift(merged(d, i), hops))
-    blocks = []
-    for d in range(nb):
-        mine = [merged(d, i) for i in range(PIECES)]
-        other = [swap(x, range(d, nb)) for x in mine]
-        blocks.append((mine, other))
-
+        for d, (bands, ks) in sets.items():
+            for i in range(len(source[d])):
+                hops = [
+                    ((b, q, c), (b, q ^ bit, c))
+                    for b in bands
+                    for k in ks
+                    for q in range(nq)
+                    for c in range(2)
+                    if (q ^ (b - k)) & (2 * bit - 1) == 0
+                    and (k or c * (n // 2) < bounds(d, n)[i + 1])
+                ]
+                give = source[d][i]
+                if t:
+                    rules = [taken(ks, u, bit, nq) for u in range(-1, t)]
+                    give = choose(rules, [[give]] + [[x] for x in got[d][i]])
+                got[d][i].append(shift(give, hops))
+    blocks = {}
+
+    def land(name, d, k, after):
+        rules = [taken((k,), u, 0, nq) for u in range(-1, stages(nq))]
+        arrived = [[x[u] for x in got[d]] for u in range(stages(nq))]
+        mine = choose(rules, [source[d]] + arrived, after)
+        blocks[name] = ([mine], [swap(mine, range(nb))])
+
+    land("first", "first", 0, [])
     wc = w // CHUNKS
     seen = [{} for _ in range(CHUNKS)]
     done = [[] for _ in range(CHUNKS)]
 
-    def apply(s, final, rhs, x, ks):
-        need = [blocks[s - k] for k in ks] + ([blocks[0]] if final else [])
+    def apply(s, final, rhs, x, ks, after):
+        need = [blocks[s - k] for k in ks] + ([blocks["rest" if s else "first"]] if final else [])
         return call(
-            lambda *refs: band_kernel(s, final, PIECES, len(ks), *refs),
+            lambda *refs: band_kernel(s, final, 1, len(ks), len(after), *refs),
             (n, wc),
             [rhs] + [seen[x][k, s] for k in ks],
-            flat(need),
+            flat(need) + after,
             block_scratch(len(need), len(ks), n, wc),
             6 * n * n * wc * (len(ks) + 1),
         )
 
     for s in range(nb):
+        if s:
+            land(s, "near" if s == 1 else s, s, [done[-1][s - 1]])
+        if s == 1:
+            land("rest", "near", 0, [done[-1][0]])
+        early = [psi[:, x * wc : (x + 1) * wc] for x in range(CHUNKS)]
+        if s > 1:
+            early = [apply(s, False, rhs, x, list(range(s - 1)), []) for x, rhs in enumerate(early)]
         for x in range(CHUNKS):
-            rhs = psi[:, x * wc : (x + 1) * wc]
-            if s > 1:
-                rhs = apply(s, False, rhs, x, list(range(s - 1)))
-            solved = apply(s, True, rhs, x, [s - 1] if s else [])
+            solved = apply(s, True, early[x], x, [s - 1] if s else [], early if s == nb - 1 > 1 else [])
             done[x].append(solved)
             have = {s: solved}
             for hops in routes(s, nb) if s + 1 < nb else []:
-                give = None
-                for a, _ in hops:
-                    give = have[a] if give is None else pick_band(a, have[a], give)
+                give = have[hops[0][0]]
                 took = shift(
                     give,
                     [((a, q, c), (b, q, c)) for a, b in hops for q in range(nq) for c in range(2)],

time: 447 us -> 490 us (1.096)
  waiting for transfers between devices: 238 us -> 291 us
  starting transfers between devices: 118 us -> 108 us
    ppermute x42 -> x43, waiting for transfers between devices: 238 us -> 291 us  [shift(): return lax.ppermute(x, AXES, pairs)]
    ppermute x42 -> x43, starting transfers between devices: 118 us -> 108 us  [shift(): return lax.ppermute(x, AXES, pairs)]
    pallas_call x32 -> x29, Pallas kernels: 61.8 us -> 62.9 us  [call(): pl.pallas_call(kernel, out_shape=jax.ShapeDtypeStruct(out_shape, F32), in...]
    unnamed x88 -> x76, local copies, waits for them, and re-layouts: 15.6 us -> 14.7 us
  transfers between devices with their start and end apart: 42 -> 43, of which waited for: 17 -> 18; matrix products, arithmetic and copies ran while one was open for 1% -> 0% of each run, Pallas kernels for 10% -> 9%
where the time goes in v3:
time: 490 us; the launch traced here: 489 us
  waiting for transfers between devices  291 us (59%)
  starting transfers between devices  108 us (22%)
  Pallas kernels  66 us (13%)
  local copies, waits for them, and re-layouts  17.8 us (4%)
    ppermute x43, waiting for transfers between devices, shift(): return lax.ppermute(x, AXES, pairs)  291 us
    ppermute x43, starting transfers between devices, shift(): return lax.ppermute(x, AXES, pairs)  108 us
    pallas_call x29, Pallas kernels, call(): pl.pallas_call(kernel, out_shape=jax.ShapeDtypeStruct(out_shape, F32), in...  62.9 us
    unnamed x76, local copies, waits for them, and re-layouts  14.7 us
  transfers between devices with their start and end apart: 43, of which 18 were waited for; matrix products, arithmetic and copies ran while one was open for 0% of the time, Pallas kernels for 9%

profile of v3, /device:TPU:15, one launch (start us, length us, event | category | flops | bytes accessed | tf_op | source)
XLA Modules:
  0.0 488.9 jit_solution(1970269755888877027)
XLA Ops:
  0.6 3.1 shard_map.41
  12.8 1.4 collective-permute-start.12
  14.3 31.2 %collective-permute-done.11.refs_1_.refs_3_ = f32[512,512]{1,0:T(8,128)S(1)} collective-permute-done((f32[512,512]{1,0:T(8,128)S(1)}, f32[512,512]{1,0:T(8,128)S(1)}, u32[]{:S(2)}, u32[]{:S(2)}) %collective-permute-start.11) | collective-permute-done | bytes 1048608 | tf_op jit(solution)/shard_map/ppermute | solution.py:280
  45.5 50.9 %collective-permute-start.13 = (f32[512,512]{1,0:T(8,128)S(1)}, f32[512,512]{1,0:T(8,128)S(1)}, u32[]{:S(2)}, u32[]{:S(2)}) collective-permute-start(f32[512,512]{1,0:T(8,128)S(1)} %shard_map.49), channel_id=1, source_target_pairs={{10,8},{11,9},{14,12},{15,13},{8,10},{9,11},{12,14},{13,15},{16,18... | collective-permute-start | bytes 3145736 | tf_op jit(solution)/shard_map/ppermute | solution.py:280
  98.6 20.8 %collective-permute-done.13.refs_5_ = f32[512,512]{1,0:T(8,128)S(1)} collective-permute-done((f32[512,512]{1,0:T(8,128)S(1)}, f32[512,512]{1,0:T(8,128)S(1)}, u32[]{:S(2)}, u32[]{:S(2)}) %collective-permute-start.13) | collective-permute-done | bytes 1048608 | tf_op jit(solution)/shard_map/ppermute | solution.py:280
  119.5 7.5 %collective-permute-start.14 = (f32[1024,512]{1,0:T(8,128)S(1)}, f32[1024,512]{1,0:T(8,128)S(1)}, u32[]{:S(2)}, u32[]{:S(2)}) collective-permute-start(f32[1024,512]{1,0:T(8,128)S(1)} %shard_map.51.refs_2_), channel_id=1, source_target_pairs={{0,1},{1,0},{2,3},{3,2},{4,5},{5,4},{6,7},{7,6},{8,9},{9,8},{10,11... | collective-permute-start | bytes 6291464 | tf_op jit(solution)/shard_map/ppermute | solution.py:280
  127.4 1.4 collective-permute-start.22
  128.8 1.4 collective-permute-start.23
  130.9 18.6 %collective-permute-done.22.refs_1_.refs_2_ = f32[512,512]{1,0:T(8,128)S(1)} collective-permute-done((f32[512,512]{1,0:T(8,128)S(1)}, f32[512,512]{1,0:T(8,128)S(1)}, u32[]{:S(2)}, u32[]{:S(2)}) %collective-permute-start.22) | collective-permute-done | bytes 1048608 | tf_op jit(solution)/shard_map/ppermute | solution.py:280
  149.5 1.5 collective-permute-start.24
  151.0 20.9 %collective-permute-done.23.refs_1_.refs_3_ = f32[512,512]{1,0:T(8,128)S(1)} collective-permute-done((f32[512,512]{1,0:T(8,128)S(1)}, f32[512,512]{1,0:T(8,128)S(1)}, u32[]{:S(2)}, u32[]{:S(2)}) %collective-permute-start.23) | collective-permute-done | bytes 1048608 | tf_op jit(solution)/shard_map/ppermute | solution.py:280
  176.7 18.1 %collective-permute-done.25.refs_5_ = f32[512,512]{1,0:T(8,128)S(1)} collective-permute-done((f32[512,512]{1,0:T(8,128)}, f32[512,512]{1,0:T(8,128)S(1)}, u32[]{:S(2)}, u32[]{:S(2)}) %collective-permute-start.25) | collective-permute-done | bytes 1048608 | tf_op jit(solution)/shard_map/ppermute | solution.py:280
  194.9 3.2 collective-permute-start.27
  199.6 1.6 collective-permute-start.21
  203.1 1.4 collective-permute-start.19
  208.1 1.8 collective-permute-start.9
  213.4 60.1 %collective-permute-done.19.refs_4_ = f32[512,512]{1,0:T(8,128)} collective-permute-done((f32[512,512]{1,0:T(8,128)}, f32[512,512]{1,0:T(8,128)}, u32[]{:S(2)}, u32[]{:S(2)}) %collective-permute-start.19) | collective-permute-done | bytes 1048608 | tf_op jit(solution)/shard_map/ppermute | solution.py:280
  273.5 22.4 %collective-permute-done.20.refs_5_ = f32[512,512]{1,0:T(8,128)S(1)} collective-permute-done((f32[512,512]{1,0:T(8,128)}, f32[512,512]{1,0:T(8,128)S(1)}, u32[]{:S(2)}, u32[]{:S(2)}) %collective-permute-start.20) | collective-permute-done | bytes 1048608 | tf_op jit(solution)/shard_map/ppermute | solution.py:280
  295.9 2.8 shard_map.62.refs_3_
  299.5 1.6 collective-permute-start.7
  302.5 2.2 shard_map.53
  304.7 1.6 collective-permute-start.30
  307.7 1.6 collective-permute-start.8
  309.3 18.8 %collective-permute-done.32.refs_1_ = f32[1024,256]{1,0:T(8,128)} collective-permute-done((f32[1024,256]{1,0:T(8,128)}, f32[1024,256]{1,0:T(8,128)}, u32[]{:S(2)}, u32[]{:S(2)}) %collective-permute-start.32) | collective-permute-done | bytes 1048608 | tf_op jit(solution)/shard_map/ppermute | solution.py:280
  330.6 1.6 copy-done.28
  333.5 1.6 collective-permute-start.34
  335.0 2.2 shard_map.65
  338.6 10.6 %shard_map.66.refs_7_.refs_0_ = f32[1024,256]{1,0:T(8,128)S(1)} custom-call(f32[1024,256]{1,0:T(8,128)S(1)} %copy-done.24, f32[1024,256]{1,0:T(8,128)} %collective-permute-done.32.refs_1_, f32[1024,256]{1,0:T(8,128)} %collective-permute-done.33.refs_2_, f32[1024,512]{1,0:T(8,128)} %shard_map.62.refs_3_, f32[1024,512]{1,0:T(8,128)} %collective-permute-done.29.refs_4_, ...), custom_call_target="tpu_custom_call" | custom-call | flops 4831838208 | bytes 1048576 | tf_op jit(solution)/shard_map/pallas_call | solution.py:232
  351.5 7.3 %collective-permute-done.16.refs_2_ = f32[1024,256]{1,0:T(8,128)} collective-permute-done((f32[1024,256]{1,0:T(8,128)}, f32[1024,256]{1,0:T(8,128)}, u32[]{:S(2)}, u32[]{:S(2)}) %collective-permute-start.16) | collective-permute-done | bytes 1048608 | tf_op jit(solution)/shard_map/ppermute | solution.py:280
  360.1 1.6 copy-done.30
  362.9 10.3 %shard_map.63.refs_0_.refs_6_ = f32[1024,256]{1,0:T(8,128)S(1)} custom-call(f32[1024,256]{1,0:T(8,128)S(1)} %copy-done.20, f32[1024,256]{1,0:T(8,128)S(1)} %copy-done.32, f32[1024,256]{1,0:T(8,128)} %collective-permute-done.16.refs_2_, f32[1024,512]{1,0:T(8,128)} %shard_map.62.refs_3_, f32[1024,512]{1,0:T(8,128)} %collective-permute-done.29.refs_4_, ...), custom_call_target="tpu_custom_call" | custom-call | flops 4831838208 | bytes 1048576 | tf_op jit(solution)/shard_map/pallas_call | solution.py:232
  373.2 8.9 %shard_map.68 = f32[1024,256]{1,0:T(8,128)S(1)} custom-call(f32[1024,256]{1,0:T(8,128)S(1)} %shard_map.66.refs_7_.refs_0_, f32[1024,256]{1,0:T(8,128)} %collective-permute-done.34.refs_1_, f32[1024,512]{1,0:T(8,128)S(1)} %shard_map.51.refs_2_, f32[1024,512]{1,0:T(8,128)S(1)} %copy-done.6, f32[1024,512]{1,0:T(8,128)S(1)} %copy-done.3, ...), custom_call_target="tpu_custom_call" | custom-call | flops 3221225472 | bytes 1048576 | tf_op jit(solution)/shard_map/pallas_call | solution.py:232
  382.5 13.0 %collective-permute-done.31.refs_1_ = f32[1024,256]{1,0:T(8,128)} collective-permute-done((f32[1024,256]{1,0:T(8,128)}, f32[1024,256]{1,0:T(8,128)}, u32[]{:S(2)}, u32[]{:S(2)}) %collective-permute-start.31) | collective-permute-done | bytes 1048608 | tf_op jit(solution)/shard_map/ppermute | solution.py:280
  395.5 8.9 %shard_map.67 = f32[1024,256]{1,0:T(8,128)S(1)} custom-call(f32[1024,256]{1,0:T(8,128)S(1)} %shard_map.63.refs_0_.refs_6_, f32[1024,256]{1,0:T(8,128)} %collective-permute-done.31.refs_1_, f32[1024,512]{1,0:T(8,128)S(1)} %shard_map.51.refs_2_, f32[1024,512]{1,0:T(8,128)S(1)} %copy-done.6, f32[1024,512]{1,0:T(8,128)S(1)} %copy-done.3, ...), custom_call_target="tpu_custom_call" | custom-call | flops 3221225472 | bytes 1048576 | tf_op jit(solution)/shard_map/pallas_call | solution.py:232
  404.3 1.5 select_select_fusion.1
  406.2 4.5 shard_map.69
  412.7 3.0 collective-permute-done.35
  415.7 1.5 dynamic-slice_add_fusion
  418.4 1.4 collective-permute-start.37
  421.0 21.0 %collective-permute-done.38 = f32[320,256]{1,0:T(8,128)S(1)} collective-permute-done((f32[320,256]{1,0:T(8,128)S(1)}, f32[320,256]{1,0:T(8,128)S(1)}, u32[]{:S(2)}, u32[]{:S(2)}) %collective-permute-start.38) | collective-permute-done | bytes 327712 | tf_op jit(solution)/shard_map/ppermute | solution.py:280
  442.0 4.0 collective-permute-done.37
  447.2 4.3 collective-permute-start.39
  452.7 10.4 %collective-permute-done.39 = f32[320,256]{1,0:T(8,128)S(1)} collective-permute-done((f32[320,256]{1,0:T(8,128)S(1)}, f32[320,256]{1,0:T(8,128)S(1)}, u32[]{:S(2)}, u32[]{:S(2)}) %collective-permute-start.39) | collective-permute-done | bytes 327712 | tf_op jit(solution)/shard_map/ppermute | solution.py:280
  463.2 2.0 collective-permute-done.40
  465.2 16.0 %collective-permute-done.41 = f32[320,256]{1,0:T(8,128)S(1)} collective-permute-done((f32[320,256]{1,0:T(8,128)S(1)}, f32[320,256]{1,0:T(8,128)S(1)}, u32[]{:S(2)}, u32[]{:S(2)}) %collective-permute-start.41) | collective-permute-done | bytes 327712 | tf_op jit(solution)/shard_map/ppermute | solution.py:280
  481.2 1.4 collective-permute-start.42
  482.9 2.4 collective-permute-done.42
  485.4 3.5 shard_map.70
  (160 shorter events, 48.7 us)
Async XLA Ops:
  3.7 2.1 collective-permute-start
  4.4 3.6 collective-permute-start.1
  5.1 3.7 collective-permute-start.2
  7.2 2.5 collective-permute-start.3
  8.2 1.5 collective-permute-start.4
  8.9 0.7 collective-permute-start.5
  9.9 87.7 %collective-permute-start.6 = (f32[1024,512]{1,0:T(8,128)S(1)}, f32[1024,512]{1,0:T(8,128)S(1)}, u32[]{:S(2)}, u32[]{:S(2)}) collective-permute-start(f32[1024,512]{1,0:T(8,128)S(1)} %shard_map.45.refs_1_), channel_id=1, source_target_pairs={{0,1},{1,0},{2,3},{3,2},{4,5},{5,4},{6,7},{7,6},{8,9},{9,8},{10,11... | collective-permute-start | bytes 6291464 | tf_op jit(solution)/shard_map/ppermute | solution.py:280
  10.6 2.1 collective-permute-start.10
  11.4 34.0 %collective-permute-start.11 = (f32[512,512]{1,0:T(8,128)S(1)}, f32[512,512]{1,0:T(8,128)S(1)}, u32[]{:S(2)}, u32[]{:S(2)}) collective-permute-start(f32[512,512]{1,0:T(8,128)S(1)} %shard_map.47.refs_0_.refs_1_), channel_id=1, source_target_pairs={{10,14},{11,15},{8,12},{9,13},{20,16},{21,17},{18,22},{19,23},{30,... | collective-permute-start | bytes 3145736 | tf_op jit(solution)/shard_map/ppermute | solution.py:280
  12.8 83.5 %copy-start.37 = (f32[1024,512]{1,0:T(8,128)S(1)}, f32[1024,512]{1,0:T(8,128)}, u32[]{:S(2)}) copy-start(f32[1024,512]{1,0:T(8,128)} %param.2) | copy-start | bytes 6291460
  12.8 85.7 %collective-permute-start.12 = (f32[512,512]{1,0:T(8,128)S(1)}, f32[512,512]{1,0:T(8,128)S(1)}, u32[]{:S(2)}, u32[]{:S(2)}) collective-permute-start(f32[512,512]{1,0:T(8,128)S(1)} %shard_map.48), channel_id=1, source_target_pairs={{10,8},{14,12},{8,10},{9,11},{12,14},{13,15},{16,18},{20,22},{18,1... | collective-permute-start | bytes 3145736 | tf_op jit(solution)/shard_map/ppermute | solution.py:280
  45.5 73.8 %collective-permute-start.13 = (f32[512,512]{1,0:T(8,128)S(1)}, f32[512,512]{1,0:T(8,128)S(1)}, u32[]{:S(2)}, u32[]{:S(2)}) collective-permute-start(f32[512,512]{1,0:T(8,128)S(1)} %shard_map.49), channel_id=1, source_target_pairs={{10,8},{11,9},{14,12},{15,13},{8,10},{9,11},{12,14},{13,15},{16,18... | collective-permute-start | bytes 3145736 | tf_op jit(solution)/shard_map/ppermute | solution.py:280
  119.5 54.9 %collective-permute-start.14 = (f32[1024,512]{1,0:T(8,128)S(1)}, f32[1024,512]{1,0:T(8,128)S(1)}, u32[]{:S(2)}, u32[]{:S(2)}) collective-permute-start(f32[1024,512]{1,0:T(8,128)S(1)} %shard_map.51.refs_2_), channel_id=1, source_target_pairs={{0,1},{1,0},{2,3},{3,2},{4,5},{5,4},{6,7},{7,6},{8,9},{9,8},{10,11... | collective-permute-start | bytes 6291464 | tf_op jit(solution)/shard_map/ppermute | solution.py:280
  127.1 175.4 %copy-start.2 = (f32[1024,512]{1,0:T(8,128)}, f32[1024,512]{1,0:T(8,128)S(1)}, u32[]{:S(2)}) copy-start(f32[1024,512]{1,0:T(8,128)S(1)} %shard_map.52.refs_4_) | copy-start | bytes 6291460
  127.1 47.3 %collective-permute-start.15 = (f32[1024,512]{1,0:T(8,128)S(1)}, f32[1024,512]{1,0:T(8,128)S(1)}, u32[]{:S(2)}, u32[]{:S(2)}) collective-permute-start(f32[1024,512]{1,0:T(8,128)S(1)} %shard_map.52.refs_4_), channel_id=1, source_target_pairs={{0,1},{1,0},{2,3},{3,2},{4,5},{5,4},{6,7},{7,6},{8,9},{9,8},{10,11... | collective-permute-start | bytes 6291464 | tf_op jit(solution)/shard_map/ppermute | solution.py:280
  127.4 22.1 %collective-permute-start.22 = (f32[512,512]{1,0:T(8,128)S(1)}, f32[512,512]{1,0:T(8,128)S(1)}, u32[]{:S(2)}, u32[]{:S(2)}) collective-permute-start(f32[512,512]{1,0:T(8,128)S(1)} %get-tuple-element.10.refs_0_), channel_id=1, source_target_pairs={{16,20},{17,21},{26,30},{27,31}} | collective-permute-start | bytes 3145736 | tf_op jit(solution)/shard_map/ppermute | solution.py:280
  128.8 43.2 %collective-permute-start.23 = (f32[512,512]{1,0:T(8,128)S(1)}, f32[512,512]{1,0:T(8,128)S(1)}, u32[]{:S(2)}, u32[]{:S(2)}) collective-permute-start(f32[512,512]{1,0:T(8,128)S(1)} %get-tuple-element.11.refs_0_.refs_1_), channel_id=1, source_target_pairs={{16,20},{17,21},{26,30},{27,31}} | collective-permute-start | bytes 3145736 | tf_op jit(solution)/shard_map/ppermute | solution.py:280
  130.1 44.2 %collective-permute-start.26 = (f32[1024,256]{1,0:T(8,128)S(1)}, f32[1024,256]{1,0:T(8,128)S(1)}, u32[]{:S(2)}, u32[]{:S(2)}) collective-permute-start(f32[1024,256]{1,0:T(8,128)S(1)} %shard_map.50.refs_6_), channel_id=1, source_target_pairs={{0,8},{1,9},{2,10},{3,11},{4,12},{5,13},{6,14},{7,15}} | collective-permute-start | bytes 3145736 | tf_op jit(solution)/shard_map/ppermute | solution.py:280
  149.5 27.2 %collective-permute-start.24 = (f32[512,512]{1,0:T(8,128)S(1)}, f32[512,512]{1,0:T(8,128)S(1)}, u32[]{:S(2)}, u32[]{:S(2)}) collective-permute-start(f32[512,512]{1,0:T(8,128)S(1)} %shard_map.56), channel_id=1, source_target_pairs={{16,18},{17,19},{20,22},{21,23},{26,24},{27,25},{30,28},{31,29}} | collective-permute-start | bytes 3145736 | tf_op jit(solution)/shard_map/ppermute | solution.py:280
  173.0 21.8 %collective-permute-start.25 = (f32[512,512]{1,0:T(8,128)}, f32[512,512]{1,0:T(8,128)S(1)}, u32[]{:S(2)}, u32[]{:S(2)}) collective-permute-start(f32[512,512]{1,0:T(8,128)} %shard_map.57), channel_id=1, source_target_pairs={{16,18},{17,19},{20,22},{21,23},{26,24},{27,25},{30,28},{31,29}} | collective-permute-start | bytes 3145736 | tf_op jit(solution)/shard_map/ppermute | solution.py:280
  194.9 14.9 %collective-permute-start.27 = (f32[1024,512]{1,0:T(8,128)S(1)}, f32[1024,512]{1,0:T(8,128)}, u32[]{:S(2)}, u32[]{:S(2)}) collective-permute-start(f32[1024,512]{1,0:T(8,128)S(1)} %shard_map.59.refs_2_.refs_5_), channel_id=1, source_target_pairs={{0,1},{1,0},{2,3},{3,2},{4,5},{5,4},{6,7},{7,6},{8,9},{9,8},{10,11... | collective-permute-start | bytes 6291464 | tf_op jit(solution)/shard_map/ppermute | solution.py:280
  198.2 3.8 collective-permute-start.17
  198.9 5.6 %collective-permute-start.18 = (f32[512,512]{1,0:T(8,128)S(1)}, f32[512,512]{1,0:T(8,128)S(1)}, u32[]{:S(2)}, u32[]{:S(2)}) collective-permute-start(f32[512,512]{1,0:T(8,128)S(1)} %get-tuple-element.11.refs_0_.refs_1_), channel_id=1, source_target_pairs={{24,28},{25,29}} | collective-permute-start | bytes 3145736 | tf_op jit(solution)/shard_map/ppermute | solution.py:280
  199.6 8.4 %collective-permute-start.21 = (f32[1024,256]{1,0:T(8,128)S(1)}, f32[1024,256]{1,0:T(8,128)}, u32[]{:S(2)}, u32[]{:S(2)}) collective-permute-start(f32[1024,256]{1,0:T(8,128)S(1)} %shard_map.50.refs_6_), channel_id=1, source_target_pairs={{0,16},{1,17},{2,18},{3,19},{4,20},{5,21},{6,22},{7,23}} | collective-permute-start | bytes 3145736 | tf_op jit(solution)/shard_map/ppermute | solution.py:280
  201.3 9.9 %collective-permute-start.28 = (f32[1024,256]{1,0:T(8,128)}, f32[1024,256]{1,0:T(8,128)S(1)}, u32[]{:S(2)}, u32[]{:S(2)}) collective-permute-start(f32[1024,256]{1,0:T(8,128)} %shard_map.58.refs_6_), channel_id=1, source_target_pairs={{8,16},{9,17},{10,18},{11,19},{12,20},{13,21},{14,22},{15,23}} | collective-permute-start | bytes 3145736 | tf_op jit(solution)/shard_map/ppermute | solution.py:280
  203.1 70.4 %collective-permute-start.19 = (f32[512,512]{1,0:T(8,128)}, f32[512,512]{1,0:T(8,128)}, u32[]{:S(2)}, u32[]{:S(2)}) collective-permute-start(f32[512,512]{1,0:T(8,128)} %shard_map.54), channel_id=1, source_target_pairs={{24,26},{25,27},{28,30},{29,31}} | collective-permute-start | bytes 3145736 | tf_op jit(solution)/shard_map/ppermute | solution.py:280
  205.7 90.2 %collective-permute-start.20 = (f32[512,512]{1,0:T(8,128)}, f32[512,512]{1,0:T(8,128)S(1)}, u32[]{:S(2)}, u32[]{:S(2)}) collective-permute-start(f32[512,512]{1,0:T(8,128)} %shard_map.55), channel_id=1, source_target_pairs={{24,26},{25,27},{28,30},{29,31}} | collective-permute-start | bytes 3145736 | tf_op jit(solution)/shard_map/ppermute | solution.py:280
  208.1 94.4 %collective-permute-start.9 = (f32[1024,256]{1,0:T(8,128)}, f32[1024,256]{1,0:T(8,128)}, u32[]{:S(2)}, u32[]{:S(2)}) collective-permute-start(f32[1024,256]{1,0:T(8,128)} %shard_map.46), channel_id=1, source_target_pairs={{0,8},{1,9},{2,10},{3,11},{4,12},{5,13},{6,14},{7,15}} | collective-permute-start | bytes 3145736 | tf_op jit(solution)/shard_map/ppermute | solution.py:280
  211.1 84.7 %copy-start.13 = (f32[512,512]{1,0:T(8,128)S(1)}, f32[512,512]{1,0:T(8,128)}, u32[]{:S(2)}) copy-start(f32[512,512]{1,0:T(8,128)} %copy-done.12) | copy-start | bytes 3145732
  213.4 85.2 %copy-start.14 = (f32[1024,256]{1,0:T(8,128)}, f32[1024,256]{1,0:T(8,128)S(1)}, u32[]{:S(2)}) copy-start(f32[1024,256]{1,0:T(8,128)S(1)} %shard_map.61.refs_6_) | copy-start | bytes 3145732
  213.4 89.1 %copy-start.18 = (f32[1024,256]{1,0:T(8,128)S(1)}, f32[1024,256]{1,0:T(8,128)}, u32[]{:S(2)}) copy-start(f32[1024,256]{1,0:T(8,128)} %get-tuple-element.14.refs_0_) | copy-start | bytes 3145732
  298.6 40.0 %collective-permute-start.29 = (f32[1024,512]{1,0:T(8,128)}, f32[1024,512]{1,0:T(8,128)}, u32[]{:S(2)}, u32[]{:S(2)}) collective-permute-start(f32[1024,512]{1,0:T(8,128)} %shard_map.62.refs_3_), channel_id=1, source_target_pairs={{0,1},{1,0},{2,3},{3,2},{4,5},{5,4},{6,7},{7,6},{8,9},{9,8},{10,11... | collective-permute-start | bytes 6291464 | tf_op jit(solution)/shard_map/ppermute | solution.py:280
  299.5 8.2 %collective-permute-start.7 = (f32[1024,256]{1,0:T(8,128)}, f32[1024,256]{1,0:T(8,128)}, u32[]{:S(2)}, u32[]{:S(2)}) collective-permute-start(f32[1024,256]{1,0:T(8,128)} %shard_map.46), channel_id=1, source_target_pairs={{0,16},{1,17},{2,18},{3,19},{4,20},{5,21},{6,22},{7,23}} | collective-permute-start | bytes 3145736 | tf_op jit(solution)/shard_map/ppermute | solution.py:280
  301.2 26.9 %collective-permute-start.32 = (f32[1024,256]{1,0:T(8,128)}, f32[1024,256]{1,0:T(8,128)}, u32[]{:S(2)}, u32[]{:S(2)}) collective-permute-start(f32[1024,256]{1,0:T(8,128)} %collective-permute-done.21.refs_1_), channel_id=1, source_target_pairs={{16,24},{17,25},{18,26},{19,27},{20,28},{21,29},{22,30},{23,31}} | collective-permute-start | bytes 3145736 | tf_op jit(solution)/shard_map/ppermute | solution.py:280
  304.7 28.7 %collective-permute-start.30 = (f32[1024,256]{1,0:T(8,128)}, f32[1024,256]{1,0:T(8,128)}, u32[]{:S(2)}, u32[]{:S(2)}) collective-permute-start(f32[1024,256]{1,0:T(8,128)} %shard_map.53), channel_id=1, source_target_pairs={{8,16},{9,17},{10,18},{11,19},{12,20},{13,21},{14,22},{15,23}} | collective-permute-start | bytes 3145736 | tf_op jit(solution)/shard_map/ppermute | solution.py:280
  306.4 30.9 %collective-permute-start.33 = (f32[1024,256]{1,0:T(8,128)}, f32[1024,256]{1,0:T(8,128)}, u32[]{:S(2)}, u32[]{:S(2)}) collective-permute-start(f32[1024,256]{1,0:T(8,128)} %shard_map.58.refs_6_), channel_id=1, source_target_pairs={{8,24},{9,25},{10,26},{11,27},{12,28},{13,29},{14,30},{15,31}} | collective-permute-start | bytes 3145736 | tf_op jit(solution)/shard_map/ppermute | solution.py:280
  307.7 42.8 %collective-permute-start.8 = (f32[1024,256]{1,0:T(8,128)}, f32[1024,256]{1,0:T(8,128)S(1)}, u32[]{:S(2)}, u32[]{:S(2)}) collective-permute-start(f32[1024,256]{1,0:T(8,128)} %collective-permute-done.7.refs_1_), channel_id=1, source_target_pairs={{16,24},{17,25},{18,26},{19,27},{20,28},{21,29},{22,30},{23,31}} | collective-permute-start | bytes 3145736 | tf_op jit(solution)/shard_map/ppermute | solution.py:280
  328.1 30.8 %collective-permute-start.16 = (f32[1024,256]{1,0:T(8,128)}, f32[1024,256]{1,0:T(8,128)}, u32[]{:S(2)}, u32[]{:S(2)}) collective-permute-start(f32[1024,256]{1,0:T(8,128)} %shard_map.53), channel_id=1, source_target_pairs={{8,24},{9,25},{10,26},{11,27},{12,28},{13,29},{14,30},{15,31}} | collective-permute-start | bytes 3145736 | tf_op jit(solution)/shard_map/ppermute | solution.py:280
  333.5 39.8 %collective-permute-start.34 = (f32[1024,256]{1,0:T(8,128)S(1)}, f32[1024,256]{1,0:T(8,128)}, u32[]{:S(2)}, u32[]{:S(2)}) collective-permute-start(f32[1024,256]{1,0:T(8,128)S(1)} %copy-done.15), channel_id=1, source_target_pairs={{16,24},{17,25},{18,26},{19,27},{20,28},{21,29},{22,30},{23,31}} | collective-permute-start | bytes 3145736 | tf_op jit(solution)/shard_map/ppermute | solution.py:280
  337.3 58.2 %collective-permute-start.31 = (f32[1024,256]{1,0:T(8,128)}, f32[1024,256]{1,0:T(8,128)}, u32[]{:S(2)}, u32[]{:S(2)}) collective-permute-start(f32[1024,256]{1,0:T(8,128)} %shard_map.65), channel_id=1, source_target_pairs={{16,24},{17,25},{18,26},{19,27},{20,28},{21,29},{22,30},{23,31}} | collective-permute-start | bytes 3145736 | tf_op jit(solution)/shard_map/ppermute | solution.py:280
  411.8 3.9 collective-permute-start.35
  418.3 23.8 %collective-permute-start.38 = (f32[320,256]{1,0:T(8,128)S(1)}, f32[320,256]{1,0:T(8,128)S(1)}, u32[]{:S(2)}, u32[]{:S(2)}) collective-permute-start(f32[320,256]{1,0:T(8,128)S(1)} %get-tuple-element.19), channel_id=1, source_target_pairs={{0,6},{1,7},{2,4},{3,5},{4,2},{5,3},{6,0},{7,1},{8,14},{9,15},{10,... | collective-permute-start | bytes 983048 | tf_op jit(solution)/shard_map/ppermute | solution.py:280
  418.4 27.6 %collective-permute-start.37 = (f32[320,256]{1,0:T(8,128)S(1)}, f32[320,256]{1,0:T(8,128)S(1)}, u32[]{:S(2)}, u32[]{:S(2)}) collective-permute-start(f32[320,256]{1,0:T(8,128)S(1)} %get-tuple-element.20), channel_id=1, source_target_pairs={{0,4},{1,5},{2,6},{3,7},{4,0},{5,1},{6,2},{7,3},{8,12},{9,13},{10,... | collective-permute-start | bytes 983048 | tf_op jit(solution)/shard_map/ppermute | solution.py:280
  419.8 26.2 %collective-permute-start.36 = (f32[320,256]{1,0:T(8,128)S(1)}, f32[320,256]{1,0:T(8,128)S(1)}, u32[]{:S(2)}, u32[]{:S(2)}) collective-permute-start(f32[320,256]{1,0:T(8,128)S(1)} %get-tuple-element.18), channel_id=1, source_target_pairs={{0,2},{1,3},{2,0},{3,1},{4,6},{5,7},{6,4},{7,5},{8,10},{9,11},{10,... | collective-permute-start | bytes 983048 | tf_op jit(solution)/shard_map/ppermute | solution.py:280
  447.2 16.0 %collective-permute-start.39 = (f32[320,256]{1,0:T(8,128)S(1)}, f32[320,256]{1,0:T(8,128)S(1)}, u32[]{:S(2)}, u32[]{:S(2)}) collective-permute-start(f32[320,256]{1,0:T(8,128)S(1)} %get-tuple-element.13), channel_id=1, source_target_pairs={{0,2},{1,3},{2,0},{3,1},{4,6},{5,7},{6,4},{7,5},{8,10},{9,11},{10,... | collective-permute-start | bytes 983048 | tf_op jit(solution)/shard_map/ppermute | solution.py:280
  451.5 13.7 %collective-permute-start.40 = (f32[320,256]{1,0:T(8,128)S(1)}, f32[320,256]{1,0:T(8,128)S(1)}, u32[]{:S(2)}, u32[]{:S(2)}) collective-permute-start(f32[320,256]{1,0:T(8,128)S(1)} %get-tuple-element.13), channel_id=1, source_target_pairs={{0,4},{1,5},{2,6},{3,7},{4,0},{5,1},{6,2},{7,3},{8,12},{9,13},{10,... | collective-permute-start | bytes 983048 | tf_op jit(solution)/shard_map/ppermute | solution.py:280
  451.5 29.7 %collective-permute-start.41 = (f32[320,256]{1,0:T(8,128)S(1)}, f32[320,256]{1,0:T(8,128)S(1)}, u32[]{:S(2)}, u32[]{:S(2)}) collective-permute-start(f32[320,256]{1,0:T(8,128)S(1)} %get-tuple-element.13), channel_id=1, source_target_pairs={{0,6},{1,7},{2,4},{3,5},{4,2},{5,3},{6,0},{7,1},{8,14},{9,15},{10,... | collective-permute-start | bytes 983048 | tf_op jit(solution)/shard_map/ppermute | solution.py:280
  481.2 4.1 collective-permute-start.42
  (33 other events, 218.9 us)
